TPU v7x, 256 devices: a whole 4x4x8 slice. The times are simulated.
256 devices in a mesh: dp: 8 (over z), pipe: 4 (over x), tensor: 8 (over y, core).
Axes of the slice: x: 4, y: 4, z: 8, core: 2. Of those that a mesh axis runs over, the one named last changes fastest.
Arguments:
- embeds: bfloat16 [32, 64, 4096], P('dp', 'tensor'), parts along dimension 0, may hold values from -6 to 6
- labels: int32 [32, 64], P('dp'), parts along dimension 0, may hold values from 0 to 24575
- norm_gain: float32 [4, 4096], P('pipe'), may hold values from 0.5 to 1.5
- w_query: bfloat16 [4, 4096, 2048], P('pipe', None, 'tensor'), may hold values from -0.09375 to 0.09375
- w_key: bfloat16 [4, 4096, 1024], P('pipe', None, 'tensor'), may hold values from -0.09375 to 0.09375
- w_value: bfloat16 [4, 4096, 1024], P('pipe', None, 'tensor'), may hold values from -0.09375 to 0.09375
- w_out: bfloat16 [4, 2048, 4096], P('pipe', 'tensor'), may hold values from -0.125 to 0.125
- final_gain: float32 [4096], replicated, may hold values from 0.5 to 1.5
- head_weight: bfloat16 [4096, 24576], P(None, ('pipe', 'tensor')), may hold values from -16 to 16
Outputs:
- token_loss: float32 [32, 64], P('dp', ('pipe', 'tensor')), parts along dimension 0
- scores: float32 [32], P('dp'), parts along dimension 0
There are 8 independent parts, one for each index of `dp`. A program takes and returns all parts, laid end to end along the dimension named above; an argument that names none is the same for every part. Nothing has to cross between parts.
All inputs are finite; a program needn't handle non-finite values.
Results may differ from a plain program's by a relative error of at most 0.014.
Values may be sent and summed in bfloat16 or wider, within the bound.
No kernel may reach another device: no remote copies, remote signals or barrier semaphores. Data moves between devices by JAX's collectives and lax.ppermute only.
A program may use at most 64 MiB of HBM per device.

v0:
```python
import functools
import math

import jax
import jax.numpy as jnp
from jax import lax
from jax.experimental import pallas as pl
from jax.experimental.pallas import tpu as pltpu
from jax.sharding import PartitionSpec as P

HD = 128
EPSILON = 1e-05
ROPE_BASE = 500000.0
CORES = 2
MIB = 1024 * 1024
F32, BF16 = jnp.float32, jnp.bfloat16
IN_VMEM = pl.BlockSpec(memory_space=pltpu.VMEM)
IN_SMEM = pl.BlockSpec(memory_space=pltpu.SMEM)
IN_HBM = pl.BlockSpec(memory_space=pltpu.HBM)


def sent_to_all(value, axis):
    size = lax.axis_size(axis)
    return lax.all_to_all(
        jnp.broadcast_to(value[None], (size, *value.shape)), axis, 0, 0, tiled=True
    )


def core_swap(value):
    size = lax.axis_size("tensor")
    return lax.ppermute(value, "tensor", [(t, t ^ 1) for t in range(size)])


def chip_swap(value, k):
    size = lax.axis_size("tensor")
    return lax.ppermute(value, "tensor", [(t, t ^ (CORES * k)) for t in range(size)])


def hop(value):
    size = lax.axis_size("pipe")
    return lax.ppermute(value, "pipe", [(i, i + 1) for i in range(size - 1)])


def normalize(states, gain_vec):
    values = states.astype(F32)
    return (
        values * lax.rsqrt(jnp.mean(values * values, axis=-1, keepdims=True) + EPSILON) * gain_vec
    )


def loader_kernel(*refs, plan):
    n_in = len(plan)
    ins, outs, sems = refs[:n_in], refs[n_in:-1], refs[-1]
    copies = []
    for i, (out, side, at) in enumerate(plan):
        target = outs[out].at[side, :, at : at + ins[i].shape[1]]
        copies.append(pltpu.make_async_copy(ins[i], target, sems.at[i]))
    for c in copies:
        c.start()
    for c in copies:
        c.wait()


def resident(arrays, room):
    flat = [w for sides in arrays for parts in sides for w in parts]
    plan, shapes = [], []
    for out, sides in enumerate(arrays):
        for side, parts in enumerate(sides):
            at = 0
            for w in parts:
                plan.append((out, side, at))
                at += w.shape[1]
        shapes.append(pltpu.VMEM((len(sides), sides[0][0].shape[0], at), BF16))
    return pl.pallas_call(
        functools.partial(loader_kernel, plan=plan),
        out_shape=shapes,
        in_specs=[IN_HBM] * len(flat),
        out_specs=[IN_VMEM] * len(shapes),
        scratch_shapes=[pltpu.SemaphoreType.DMA((len(flat),))],
        cost_estimate=pl.CostEstimate(
            flops=10**9, bytes_accessed=4 * sum(w.size for w in flat), transcendentals=0
        ),
        compiler_params=pltpu.CompilerParams(vmem_limit_bytes=room * MIB),
        name="resident",
    )(*flat)


def section_body(rows, context, state, w_in, w_out, cos_ref, sin_ref, bias_ref, outs):
    cosine, sine, bias = cos_ref[...], sin_ref[...], bias_ref[...]
    n_rows = rows.shape[0]
    sides, depth, _ = w_out.shape

    def rotated(t):
        return (t * cosine + pltpu.roll(t, HD // 2, 1) * sine).astype(BF16)

    def attend(side, carry):
        both = jnp.dot(rows[...], w_in[side], preferred_element_type=F32)
        heads = both.shape[1] // HD - 2
        keys = rotated(both[:, heads * HD : (heads + 1) * HD])
        values = both[:, (heads + 1) * HD :].astype(BF16)
        stacked = jnp.concatenate(
            [rotated(both[:, h * HD : (h + 1) * HD]) for h in range(heads)], axis=0
        )
        logits = lax.dot_general(
            stacked, keys, (((1,), (1,)), ((), ())), preferred_element_type=F32
        ) / math.sqrt(HD)
        logits = logits + bias
        weights = jnp.exp(logits - jnp.max(logits, axis=-1, keepdims=True))
        probs = (weights / jnp.sum(weights, axis=-1, keepdims=True)).astype(BF16)
        out = jnp.dot(probs, values, preferred_element_type=F32).astype(BF16)
        context[side] = jnp.concatenate(
            [out[h * n_rows : (h + 1) * n_rows] for h in range(heads)], axis=1
        )
        return carry

    lax.fori_loop(0, sides, attend, 0)
    block, width = outs[0].shape
    step = width // 2

    def columns(c, carry):
        cols = pl.ds(pl.multiple_of(c * step, step), step)
        part = sum(
            jnp.dot(context[i], w_out[i, :, cols], preferred_element_type=F32)
            for i in range(sides)
        )
        outs[0][:, cols] = part[:block] + state[:, cols].astype(F32)
        for i in range(1, len(outs)):
            outs[i][:, cols] = part[i * block : (i + 1) * block].astype(BF16)
        return carry

    lax.fori_loop(0, width // step, columns, 0)


def section_kernel(r0, r1, r2, r3, state, *rest):
    *rest, rows, context = rest
    block = r0.shape[0]
    for i, r in enumerate((r0, r1, r2, r3)):
        rows[i * block : (i + 1) * block, :] = r[...]
    section_body(rows, context, state, *rest[:5], rest[5:])


def first_kernel(at_ref, whole, gain_ref, *rest):
    *rest, rows, context, state = rest
    chips = 4
    block = whole.shape[0] // chips
    for k in range(chips):
        row = jnp.bitwise_xor(at_ref[0], k) * block
        values = whole[pl.ds(pl.multiple_of(row, block), block), :]
        if k == 0:
            state[...] = values
        values = values.astype(F32)
        mean = jnp.mean(values * values, axis=-1, keepdims=True)
        normed = values * lax.rsqrt(mean + EPSILON) * gain_ref[...]
        rows[k * block : (k + 1) * block, :] = normed.astype(BF16)
    section_body(rows, context, state, *rest[:5], rest[5:])


def section_block(kernel, specs, entering, block, width, held, tables, scratch=()):
    shapes = [jax.ShapeDtypeStruct((block, width), F32)] + [
        jax.ShapeDtypeStruct((block, width), BF16)
    ] * 3
    n_rows = tables[0].shape[0]
    sides, depth, _ = held[1].shape
    return pl.pallas_call(
        kernel,
        out_shape=shapes,
        in_specs=specs + [IN_VMEM] * 5,
        out_specs=[IN_VMEM] * 4,
        scratch_shapes=[
            pltpu.VMEM((n_rows, width), BF16),
            pltpu.VMEM((sides, n_rows, depth), BF16),
            *scratch,
        ],
        cost_estimate=pl.CostEstimate(
            flops=8 * 10**9, bytes_accessed=2 * width * 1536, transcendentals=0
        ),
        compiler_params=pltpu.CompilerParams(vmem_limit_bytes=16 * MIB),
        name="section_block",
    )(*entering, *held, *tables)


def as_column(row):
    n = row.shape[1]
    return jnp.transpose(jnp.broadcast_to(row, (n, n)))[:, :1]


def head_kernel(
    at_ref, mine, theirs, w_ref, ids_ref, logits_ref, stats_ref, gram_ref, hidden
):
    chip, core = at_ref[0], at_ref[1]
    chips = 4
    block = mine.shape[0] // chips
    for side, rows in ((core, mine), (1 - core, theirs)):
        for k in range(chips):
            row = (side * chips + jnp.bitwise_xor(chip, k)) * block
            target = pl.ds(pl.multiple_of(row, block), block)
            hidden[target, :] = rows[k * block : (k + 1) * block, :]
    step = 256

    def columns(c, carry):
        cols = pl.ds(pl.multiple_of(c * step, step), step)
        logits_ref[:, cols] = jnp.dot(hidden[...], w_ref[0, :, cols], preferred_element_type=F32)
        return carry

    lax.fori_loop(0, w_ref.shape[2] // step, columns, 0)
    logits = logits_ref[...]
    n_rows, vocab = logits.shape
    hit = as_column(ids_ref[...]) == lax.broadcasted_iota(jnp.int32, (n_rows, vocab), 1).astype(F32)
    target = jnp.sum(jnp.where(hit, logits, 0.0), axis=1, keepdims=True)
    peak = jnp.max(logits, axis=1, keepdims=True)
    total = jnp.sum(jnp.exp(logits - peak), axis=1, keepdims=True)
    lane = lax.broadcasted_iota(jnp.int32, (n_rows, n_rows), 1)
    table = jnp.where(lane == 0, peak, jnp.where(lane == 1, total, target))
    stats_ref[...] = jnp.transpose(table)[:8]
    seq = n_rows // CORES
    for i in range(CORES):
        h = hidden[i * seq : (i + 1) * seq, :]
        gram_ref[i] = lax.dot_general(h, h, (((1,), (1,)), ((), ())), preferred_element_type=F32)


def head_block(where, mine, theirs, head_weight, ids):
    seq, width = mine.shape
    n_rows, vocab = CORES * seq, head_weight.shape[2]
    return pl.pallas_call(
        head_kernel,
        out_shape=[
            jax.ShapeDtypeStruct((n_rows, vocab), F32),
            jax.ShapeDtypeStruct((8, n_rows), F32),
            jax.ShapeDtypeStruct((CORES, seq, seq), F32),
        ],
        in_specs=[IN_SMEM] + [IN_VMEM] * 4,
        out_specs=[IN_VMEM] * 3,
        scratch_shapes=[pltpu.VMEM((n_rows, width), BF16)],
        cost_estimate=pl.CostEstimate(
            flops=4 * 10**9, bytes_accessed=2 * width * vocab, transcendentals=0
        ),
        compiler_params=pltpu.CompilerParams(vmem_limit_bytes=16 * MIB),
        name="head_block",
    )(where, mine, theirs, head_weight, ids)


def score_kernel(l0, l1, norm_ref, i0, i1, g0, g1, out_ref):
    chain_rows, vocab = l0.shape
    seq = chain_rows // CORES
    lane = lax.broadcasted_iota(jnp.int32, (8, 128), 1)
    result = jnp.zeros((8, 128), F32)
    for j, (logits, ids, gram) in enumerate(((l0, i0, g0), (l1, i1, g1))):
        norm = as_column(norm_ref[:, j * chain_rows : (j + 1) * chain_rows])
        entry = lax.broadcasted_iota(jnp.int32, (chain_rows, vocab), 1).astype(F32)
        hit = as_column(ids[...]) == entry
        errors = jnp.exp(logits[...] - norm) - hit.astype(F32)
        errors = errors.astype(BF16)
        for i in range(CORES):
            e = errors[i * seq : (i + 1) * seq]
            pair = lax.dot_general(e, e, (((1,), (1,)), ((), ())), preferred_element_type=F32)
            result = jnp.where(lane == j * CORES + i, jnp.sum(pair * gram[i]), result)
    out_ref[...] = result


def score_block(logits, log_norm, ids, grams):
    return pl.pallas_call(
        score_kernel,
        out_shape=jax.ShapeDtypeStruct((8, 128), F32),
        in_specs=[IN_VMEM] * 7,
        out_specs=IN_VMEM,
        cost_estimate=pl.CostEstimate(flops=10**9, bytes_accessed=10**6, transcendentals=0),
        compiler_params=pltpu.CompilerParams(vmem_limit_bytes=12 * MIB),
        name="score_block",
    )(*logits, log_norm, *ids, *grams)


def per_device(embeds, labels, norm_gain, w_query, w_key, w_value, w_out, final_gain, head_weight):
    pipe_count = lax.axis_size("pipe")
    tensor_count = lax.axis_size("tensor")
    chips = tensor_count // CORES
    section = lax.axis_index("pipe")
    rank = lax.axis_index("tensor")
    chip, core = rank // CORES, rank % CORES
    micro, own_rows, width = embeds.shape
    chains = micro // CORES
    seq_len = own_rows * tensor_count
    block = own_rows * CORES

    own_w = (w_query[0], w_key[0], w_value[0], w_out[0])
    vocab_dev = head_weight.shape[1]
    slot = section * tensor_count + rank
    loss_width = seq_len // (pipe_count * tensor_count)
    at_section = [section == p for p in range(pipe_count - 1)]
    scalars = (core == 0, at_section, slot * vocab_dev, slot * loss_width, chip, core)
    embeds, scalars = lax.optimization_barrier((embeds, scalars))
    on_first, at_section, first_id, loss_at, chip, core = scalars
    ids = (labels - first_id).astype(F32).reshape(chains, 1, CORES * seq_len)
    where = jnp.stack([chip, core]).astype(jnp.int32)

    first_rows = jnp.broadcast_to(embeds[:CORES][None], (chips, CORES, own_rows, width))
    first_rows = first_rows.reshape(tensor_count, own_rows, width)
    whole = lax.all_to_all(first_rows, "tensor", 0, 0, tiled=True).reshape(seq_len, width)
    other_w = [core_swap(w) for w in own_w]

    later = embeds[CORES:].reshape(chains - 1, CORES, own_rows, width)
    mine = jnp.where(on_first, later[:, 0], later[:, 1])
    got = core_swap(jnp.where(on_first, later[:, 1], later[:, 0]))
    start = jnp.where(
        on_first, jnp.concatenate([mine, got], axis=1), jnp.concatenate([got, mine], axis=1)
    )

    at = jnp.arange(seq_len, dtype=jnp.int32)
    place = jnp.bitwise_xor(chip, at // block) * block + at % block
    half = HD // 2
    inverse = ROPE_BASE ** (-2.0 * jnp.arange(half, dtype=F32) / HD)
    angles = place.astype(F32)[:, None] * inverse[None, :]
    cosine, sine = jnp.cos(angles), jnp.sin(angles)
    cosine = jnp.concatenate([cosine, cosine], axis=1)
    sine = jnp.concatenate([-sine, sine], axis=1)
    bias = jnp.where(place[:, None] >= place[None, :], 0.0, -1e30)
    bias = jnp.concatenate([bias] * (own_w[0].shape[1] // HD), axis=0)

    def gathered(rows):
        return [rows] + [chip_swap(rows, k) for k in range(1, chips)]

    tables = (cosine, sine, bias)
    ready = lax.optimization_barrier((whole, [*ids], where, tables, own_w))
    whole, ids, where, tables, own_w = ready
    held = resident(
        [[own_w[:3], other_w[:3]], [own_w[3:], other_w[3:]]],
        48,
    )

    def summed(parts, after=()):
        got = [chip_swap(parts[k], k) for k in range(1, chips)]
        got, after = lax.optimization_barrier((got, after))
        total = parts[0]
        for g in got:
            total = total + g.astype(F32)
        return total.astype(BF16), after

    def section_tick(state, normed, tick, beside=(), after=()):
        with jax.named_scope(f"tick{tick}"):
            blocks = gathered(normed)
            blocks, beside = lax.optimization_barrier((blocks, beside))
            after = after(beside) if after else ()
            parts = section_block(
                section_kernel,
                [IN_VMEM] * 5,
                (*blocks, state),
                block,
                width,
                held,
                tables,
            )
            return (*summed(parts, after), beside)

    def next_state(result, tick):
        with jax.named_scope(f"hop{tick}"):
            state = hop(result)
            if tick < chains:
                state = jnp.where(at_section[0], start[tick - 1], state)
            return state, normalize(state, norm_gain[0]).astype(BF16)

    def spread_of(result, j):
        with jax.named_scope(f"spread{j}"):
            hidden = normalize(result, final_gain).astype(BF16)
            here = [
                lax.ppermute(hidden, "pipe", [(pipe_count - 1, p)]) for p in range(pipe_count - 1)
            ]
            spread = hidden
            for p in range(pipe_count - 1):
                spread = jnp.where(at_section[p], here[p], spread)
            return spread

    with jax.named_scope("tick0"):
        parts = section_block(
            first_kernel,
            [IN_SMEM, IN_VMEM, IN_VMEM],
            (where, whole, norm_gain),
            block,
            width,
            held,
            tables,
            scratch=[pltpu.VMEM((block, width), BF16)],
        )
        result, _ = summed(parts)
    ticks = chains + pipe_count - 1
    heads = []
    for tick in range(1, ticks):
        state, normed = next_state(result, tick)
        if tick == 1:
            normed, late = lax.optimization_barrier((normed, head_weight))
            (head_w,) = resident([[[late]]], 24)
            result, _, head_w = section_tick(state, normed, tick, beside=head_w)
            continue
        if tick < ticks - 1:
            result, _, _ = section_tick(state, normed, tick)
            continue
        done, normed = lax.optimization_barrier((result, normed))
        spread = spread_of(done, 0)
        result, blocks, _ = section_tick(
            state, normed, tick, beside=spread, after=lambda s: gathered(s)
        )
        with jax.named_scope("head0"):
            full = jnp.concatenate(blocks, axis=0)
            first = (full, core_swap(full))
    spread = spread_of(result, 1)
    spread, first = lax.optimization_barrier((spread, first))
    heads.append(head_block(where, *first, head_w, ids[0]))
    with jax.named_scope("head1"):
        blocks = gathered(spread)
        blocks, heads = lax.optimization_barrier((blocks, heads))
        full = jnp.concatenate(blocks, axis=0)
        heads.append(head_block(where, full, core_swap(full), head_w, ids[1]))

    with jax.named_scope("scores"):
        stats = jnp.concatenate([h[1] for h in heads], axis=1)[:3]
        stats = sent_to_all(stats, ("pipe", "tensor"))
        peak = jnp.max(stats[:, 0], axis=0)
        exp_total = jnp.sum(stats[:, 1] * jnp.exp(stats[:, 0] - peak), axis=0)
        target = jnp.sum(stats[:, 2], axis=0)
        log_norm = peak + jnp.log(exp_total)
        parts = score_block(
            [h[0] for h in heads], log_norm[None], ids, [h[2] for h in heads]
        )
        totals = sent_to_all(parts[:1, :micro], ("pipe", "tensor")).sum(axis=(0, 1))
        scores = jnp.sqrt(totals) / seq_len
        losses = (log_norm - target).reshape(micro, seq_len)
        token_loss = lax.dynamic_slice(
            losses, (0, loss_at), (micro, loss_width), allow_negative_indices=False
        )
    return (token_loss, scores)


def solution(mesh):
    in_specs = (
        P("dp", "tensor", None),
        P("dp", None),
        P("pipe", None),
        P("pipe", None, "tensor"),
        P("pipe", None, "tensor"),
        P("pipe", None, "tensor"),
        P("pipe", "tensor", None),
        P(),
        P(None, ("pipe", "tensor")),
    )
    out_specs = (P("dp", ("pipe", "tensor")), P("dp"))
    return jax.shard_map(
        per_device, mesh=mesh, in_specs=in_specs, out_specs=out_specs, check_vma=False
    )
```

profile of v0, /device:TPU:1, one launch (start us, length us, event | category | flops | bytes accessed | tf_op | source)
XLA Modules:
  0.0 217.3 jit_solution(6847596964893032698)
XLA Ops:
  0.6 3.3 %collective-permute-start.1 = (bf16[4096,256]{1,0:T(8,128)(2,1)}, bf16[4096,256]{1,0:T(8,128)(2,1)S(1)}, u32[]{:S(2)}, u32[]{:S(2)}) collective-permute-start(bf16[4096,256]{1,0:T(8,128)(2,1)} %bitcast.39), channel_id=1, source_target_pairs={{0,1},{1,0},{2,3},{3,2},{4,5},{5,4},{6,7},{7,6},{8,9},{9,8},{10,11... | collective-permute-start | bytes 6291464 | tf_op jit(solution)/shard_map/ppermute | solution.py:31
  5.9 3.8 %all-to-all-start = ((bf16[8,8,4096]{2,1,0:T(8,128)(2,1)}), bf16[8,8,4096]{2,1,0:T(8,128)(2,1)S(1)}, u32[]{:S(2)}, u32[]{:S(2)}) async-start(bf16[8,8,4096]{2,1,0:T(8,128)(2,1)} %bitcast.4), calls=%async_computation | async-start | bytes 1048576 | tf_op jit(solution)/shard_map/all_to_all | solution.py:297
  11.6 7.5 %all-to-all-done = bf16[8,8,4096]{2,1,0:T(8,128)(2,1)S(1)} async-done(((bf16[8,8,4096]{2,1,0:T(8,128)(2,1)}), bf16[8,8,4096]{2,1,0:T(8,128)(2,1)S(1)}, u32[]{:S(2)}, u32[]{:S(2)}) %all-to-all-start) | async-done | bytes 524320 | tf_op jit(solution)/shard_map/all_to_all | solution.py:297
  19.1 1.3 copy-done.1
  20.4 4.7 %resident.2 = (bf16[2,4096,512]{2,1,0:T(8,128)(2,1)S(1)}, bf16[2,256,4096]{2,1,0:T(8,128)(2,1)S(1)}) custom-call(bf16[4096,256]{1,0:T(8,128)(2,1)} %bitcast.40, bf16[4096,128]{1,0:T(8,128)(2,1)} %bitcast.44, bf16[4096,128]{1,0:T(8,128)(2,1)} %bitcast.46, bf16[4096,256]{1,0:T(8,128)(2,1)} %copy-done.1, bf16[4096,128]{1,0:T(8,128)(2,1)} %collective-permute-done.2.refs_4_, ...), custom_call_target="tpu_custom_call" | custom-call | flops 1000000000 | bytes 25165824 | tf_op jit(solution)/shard_map/resident/pallas_call | solution.py:74
  25.2 4.5 %section_block.5 = (f32[16,4096]{1,0:T(8,128)S(1)}, bf16[16,4096]{1,0:T(8,128)(2,1)S(1)}, bf16[16,4096]{1,0:T(8,128)(2,1)S(1)}, bf16[16,4096]{1,0:T(8,128)(2,1)S(1)}) custom-call(s32[2]{0:T(128)S(1)} %pad_add_fusion.at_ref, bf16[64,4096]{1,0:T(8,128)(2,1)S(1)} %bitcast.33, f32[1,4096]{1,0:T(1,128)S(1)} %copy-done, ...), custom_call_target="tpu_custom_call" | custom-call | flops 8000000000 | bytes 12582912 | tf_op jit(solution)/shard_map/tick0/section_block/pallas_call | solution.py:164
  30.0 1.8 collective-permute-start.6
  31.8 1.8 collective-permute-start.7
  33.6 3.3 %collective-permute-done.6 = bf16[16,4096]{1,0:T(8,128)(2,1)S(1)} collective-permute-done((bf16[16,4096]{1,0:T(8,128)(2,1)S(1)}, bf16[16,4096]{1,0:T(8,128)(2,1)S(1)}, u32[]{:S(2)}, u32[]{:S(2)}) %collective-permute-start.6) | collective-permute-done | bytes 131104 | tf_op jit(solution)/shard_map/tick0/ppermute | solution.py:36
  36.9 2.9 %collective-permute-done.7 = bf16[16,4096]{1,0:T(8,128)(2,1)S(1)} collective-permute-done((bf16[16,4096]{1,0:T(8,128)(2,1)S(1)}, bf16[16,4096]{1,0:T(8,128)(2,1)S(1)}, u32[]{:S(2)}, u32[]{:S(2)}) %collective-permute-start.7) | collective-permute-done | bytes 131104 | tf_op jit(solution)/shard_map/tick0/ppermute | solution.py:36
  39.9 2.5 %collective-permute-start.8 = (bf16[16,4096]{1,0:T(8,128)(2,1)S(1)}, bf16[16,4096]{1,0:T(8,128)(2,1)S(1)}, u32[]{:S(2)}, u32[]{:S(2)}) collective-permute-start(bf16[16,4096]{1,0:T(8,128)(2,1)S(1)} %add_convert_fusion.4), channel_id=1, source_target_pairs={{0,8},{8,16},{16,24},{1,9},{9,17},{17,25},{2,10},{10,18},{18,26},{... | collective-permute-start | bytes 393224 | tf_op jit(solution)/shard_map/hop1/ppermute | solution.py:41
  42.4 1.6 collective-permute-start
  45.2 1.9 collective-permute-start.11
  47.1 1.5 collective-permute-start.9
  49.0 1.3 collective-permute-done.11.r3
  50.3 2.2 %collective-permute-done.10.r2 = bf16[16,4096]{1,0:T(8,128)(2,1)S(1)} collective-permute-done((bf16[16,4096]{1,0:T(8,128)(2,1)S(1)}, bf16[16,4096]{1,0:T(8,128)(2,1)S(1)}, u32[]{:S(2)}, u32[]{:S(2)}) %collective-permute-start.10) | collective-permute-done | bytes 131104 | tf_op jit(solution)/shard_map/tick1/ppermute | solution.py:36
  53.3 3.7 %section_block.6 = (f32[16,4096]{1,0:T(8,128)S(1)}, bf16[16,4096]{1,0:T(8,128)(2,1)S(1)}, bf16[16,4096]{1,0:T(8,128)(2,1)S(1)}, bf16[16,4096]{1,0:T(8,128)(2,1)S(1)}) custom-call(bf16[16,4096]{1,0:T(8,128)(2,1)S(1)} %fusion.2.r0, bf16[16,4096]{1,0:T(8,128)(2,1)S(1)} %collective-permute-done.9.r1, bf16[16,4096]{1,0:T(8,128)(2,1)S(1)} %collective-permute-done.10.r2, ...), custom_call_target="tpu_custom_call" | custom-call | flops 8000000000 | bytes 12582912 | tf_op jit(solution)/shard_map/tick1/section_block/pallas_call | solution.py:164
  57.4 2.7 %collective-permute-start.13 = (bf16[16,4096]{1,0:T(8,128)(2,1)S(1)}, bf16[16,4096]{1,0:T(8,128)(2,1)S(1)}, u32[]{:S(2)}, u32[]{:S(2)}) collective-permute-start(bf16[16,4096]{1,0:T(8,128)(2,1)S(1)} %get-tuple-element.134), channel_id=1, source_target_pairs={{0,4},{1,5},{2,6},{3,7},{4,0},{5,1},{6,2},{7,3},{8,12},{9,13},{10,... | collective-permute-start | bytes 393224 | tf_op jit(solution)/shard_map/tick1/ppermute | solution.py:36
  60.9 2.9 %collective-permute-done.13 = bf16[16,4096]{1,0:T(8,128)(2,1)S(1)} collective-permute-done((bf16[16,4096]{1,0:T(8,128)(2,1)S(1)}, bf16[16,4096]{1,0:T(8,128)(2,1)S(1)}, u32[]{:S(2)}, u32[]{:S(2)}) %collective-permute-start.13) | collective-permute-done | bytes 131104 | tf_op jit(solution)/shard_map/tick1/ppermute | solution.py:36
  63.8 1.4 collective-permute-done.14
  65.3 2.5 %collective-permute-start.15 = (bf16[16,4096]{1,0:T(8,128)(2,1)S(1)}, bf16[16,4096]{1,0:T(8,128)(2,1)S(1)}, u32[]{:S(2)}, u32[]{:S(2)}) collective-permute-start(bf16[16,4096]{1,0:T(8,128)(2,1)S(1)} %add_convert_fusion.3), channel_id=1, source_target_pairs={{0,8},{8,16},{16,24},{1,9},{9,17},{17,25},{2,10},{10,18},{18,26},{... | collective-permute-start | bytes 393224 | tf_op jit(solution)/shard_map/hop2/ppermute | solution.py:41
  67.7 1.9 collective-permute-done.15.state
  71.1 1.1 collective-permute-start.17
  73.3 1.8 collective-permute-done.18.r3
  75.1 1.4 collective-permute-done.17.r2
  77.0 3.7 %section_block.7 = (f32[16,4096]{1,0:T(8,128)S(1)}, bf16[16,4096]{1,0:T(8,128)(2,1)S(1)}, bf16[16,4096]{1,0:T(8,128)(2,1)S(1)}, bf16[16,4096]{1,0:T(8,128)(2,1)S(1)}) custom-call(bf16[16,4096]{1,0:T(8,128)(2,1)S(1)} %fusion.5.r0, bf16[16,4096]{1,0:T(8,128)(2,1)S(1)} %collective-permute-done.16.r1, bf16[16,4096]{1,0:T(8,128)(2,1)S(1)} %collective-permute-done.17.r2, ...), custom_call_target="tpu_custom_call" | custom-call | flops 8000000000 | bytes 12582912 | tf_op jit(solution)/shard_map/tick2/section_block/pallas_call | solution.py:164
  81.2 1.8 collective-permute-start.20
  83.0 1.6 collective-permute-start.21
  85.2 2.2 %collective-permute-done.20 = bf16[16,4096]{1,0:T(8,128)(2,1)S(1)} collective-permute-done((bf16[16,4096]{1,0:T(8,128)(2,1)S(1)}, bf16[16,4096]{1,0:T(8,128)(2,1)S(1)}, u32[]{:S(2)}, u32[]{:S(2)}) %collective-permute-start.20) | collective-permute-done | bytes 131104 | tf_op jit(solution)/shard_map/tick2/ppermute | solution.py:36
  87.3 1.3 collective-permute-done.21
  88.8 4.1 %collective-permute-start.22 = (bf16[16,4096]{1,0:T(8,128)(2,1)S(1)}, bf16[16,4096]{1,0:T(8,128)(2,1)S(1)}, u32[]{:S(2)}, u32[]{:S(2)}) collective-permute-start(bf16[16,4096]{1,0:T(8,128)(2,1)S(1)} %add_convert_fusion.2), channel_id=1, source_target_pairs={{0,8},{8,16},{16,24},{1,9},{9,17},{17,25},{2,10},{10,18},{18,26},{... | collective-permute-start | bytes 393224 | tf_op jit(solution)/shard_map/hop3/ppermute | solution.py:41
  92.8 1.9 collective-permute-done.22.state
  95.0 1.8 collective-permute-start.25
  96.8 1.6 collective-permute-start.23
  98.4 1.8 collective-permute-done.25.r3
  100.2 2.0 collective-permute-done.24.r2
  102.2 3.7 %section_block.8 = (f32[16,4096]{1,0:T(8,128)S(1)}, bf16[16,4096]{1,0:T(8,128)(2,1)S(1)}, bf16[16,4096]{1,0:T(8,128)(2,1)S(1)}, bf16[16,4096]{1,0:T(8,128)(2,1)S(1)}) custom-call(bf16[16,4096]{1,0:T(8,128)(2,1)S(1)} %fusion.8.r0, bf16[16,4096]{1,0:T(8,128)(2,1)S(1)} %collective-permute-done.23.r1, bf16[16,4096]{1,0:T(8,128)(2,1)S(1)} %collective-permute-done.24.r2, ...), custom_call_target="tpu_custom_call" | custom-call | flops 8000000000 | bytes 12582912 | tf_op jit(solution)/shard_map/tick3/section_block/pallas_call | solution.py:164
  106.0 2.8 %collective-permute-start.27 = (bf16[16,4096]{1,0:T(8,128)(2,1)S(1)}, bf16[16,4096]{1,0:T(8,128)(2,1)S(1)}, u32[]{:S(2)}, u32[]{:S(2)}) collective-permute-start(bf16[16,4096]{1,0:T(8,128)(2,1)S(1)} %get-tuple-element.156), channel_id=1, source_target_pairs={{0,4},{1,5},{2,6},{3,7},{4,0},{5,1},{6,2},{7,3},{8,12},{9,13},{10,... | collective-permute-start | bytes 393224 | tf_op jit(solution)/shard_map/tick3/ppermute | solution.py:36
  110.1 3.7 %collective-permute-done.27 = bf16[16,4096]{1,0:T(8,128)(2,1)S(1)} collective-permute-done((bf16[16,4096]{1,0:T(8,128)(2,1)S(1)}, bf16[16,4096]{1,0:T(8,128)(2,1)S(1)}, u32[]{:S(2)}, u32[]{:S(2)}) %collective-permute-start.27) | collective-permute-done | bytes 131104 | tf_op jit(solution)/shard_map/tick3/ppermute | solution.py:36
  113.7 1.6 collective-permute-done.28
  115.4 4.1 %collective-permute-start.29 = (bf16[16,4096]{1,0:T(8,128)(2,1)S(1)}, bf16[16,4096]{1,0:T(8,128)(2,1)S(1)}, u32[]{:S(2)}, u32[]{:S(2)}) collective-permute-start(bf16[16,4096]{1,0:T(8,128)(2,1)S(1)} %add_convert_fusion.1), channel_id=1, source_target_pairs={{0,8},{8,16},{16,24},{1,9},{9,17},{17,25},{2,10},{10,18},{18,26},{... | collective-permute-start | bytes 393224 | tf_op jit(solution)/shard_map/hop4/ppermute | solution.py:41
  119.5 1.9 collective-permute-done.29.state
  122.0 1.3 collective-permute-start.35
  124.6 1.4 collective-permute-start.32
  126.3 2.5 %collective-permute-done.35 = bf16[16,4096]{1,0:T(8,128)(2,1)S(1)} collective-permute-done((bf16[16,4096]{1,0:T(8,128)(2,1)S(1)}, bf16[16,4096]{1,0:T(8,128)(2,1)S(1)}, u32[]{:S(2)}, u32[]{:S(2)}) %collective-permute-start.35) | collective-permute-done | bytes 131104 | tf_op jit(solution)/shard_map/spread0/ppermute | solution.py:364
  129.7 1.6 collective-permute-done.31.r2
  131.3 1.4 collective-permute-done.30.r1
  132.7 3.7 %section_block.9 = (f32[16,4096]{1,0:T(8,128)S(1)}, bf16[16,4096]{1,0:T(8,128)(2,1)S(1)}, bf16[16,4096]{1,0:T(8,128)(2,1)S(1)}, bf16[16,4096]{1,0:T(8,128)(2,1)S(1)}) custom-call(bf16[16,4096]{1,0:T(8,128)(2,1)S(1)} %fusion.11.r0, bf16[16,4096]{1,0:T(8,128)(2,1)S(1)} %collective-permute-done.30.r1, bf16[16,4096]{1,0:T(8,128)(2,1)S(1)} %collective-permute-done.31.r2, ...), custom_call_target="tpu_custom_call" | custom-call | flops 8000000000 | bytes 12582912 | tf_op jit(solution)/shard_map/tick4/section_block/pallas_call | solution.py:164
  136.5 2.5 %collective-permute-start.37 = (bf16[16,4096]{1,0:T(8,128)(2,1)S(1)}, bf16[16,4096]{1,0:T(8,128)(2,1)S(1)}, u32[]{:S(2)}, u32[]{:S(2)}) collective-permute-start(bf16[16,4096]{1,0:T(8,128)(2,1)S(1)} %get-tuple-element.170), channel_id=1, source_target_pairs={{0,4},{1,5},{2,6},{3,7},{4,0},{5,1},{6,2},{7,3},{8,12},{9,13},{10,... | collective-permute-start | bytes 393224 | tf_op jit(solution)/shard_map/tick4/ppermute | solution.py:36
  139.0 1.3 collective-permute-start.38
  140.3 1.3 collective-permute-start.41
  141.7 1.9 collective-permute-start.39
  143.6 5.0 %collective-permute-done.38 = bf16[16,4096]{1,0:T(8,128)(2,1)S(1)} collective-permute-done((bf16[16,4096]{1,0:T(8,128)(2,1)S(1)}, bf16[16,4096]{1,0:T(8,128)(2,1)S(1)}, u32[]{:S(2)}, u32[]{:S(2)}) %collective-permute-start.38) | collective-permute-done | bytes 131104 | tf_op jit(solution)/shard_map/tick4/ppermute | solution.py:36
  150.1 1.3 collective-permute-start.44
  152.8 16.7 %collective-permute-start.45 = (bf16[64,4096]{1,0:T(8,128)(2,1)S(1)}, bf16[64,4096]{1,0:T(8,128)(2,1)S(1)}, u32[]{:S(2)}, u32[]{:S(2)}) collective-permute-start(bf16[64,4096]{1,0:T(8,128)(2,1)S(1)} %constant_dynamic-update-slice_fusion.mine), channel_id=1, source_target_pairs={{0,1},{1,0},{2,3},{3,2},{4,5},{5,4},{6,7},{7,6},{8,9},{9,8},{10,11... | collective-permute-start | bytes 1572872 | tf_op jit(solution)/shard_map/head0/ppermute | solution.py:31
  169.7 1.4 collective-permute-done.45.theirs
  171.1 1.2 collective-permute-start.48
  174.3 2.4 %head_block.2 = (f32[128,768]{1,0:T(8,128)S(1)}, f32[8,128]{1,0:T(8,128)S(1)}, f32[2,64,64]{2,1,0:T(8,128)S(1)}) custom-call(s32[2]{0:T(128)S(1)} %pad_add_fusion.at_ref, bf16[64,4096]{1,0:T(8,128)(2,1)S(1)} %constant_dynamic-update-slice_fusion.mine, bf16[64,4096]{1,0:T(8,128)(2,1)S(1)} %collective-permute-done.45.theirs, ...), custom_call_target="tpu_custom_call" | custom-call | flops 4000000000 | bytes 6291456 | tf_op jit(solution)/shard_map/head_block/pallas_call | solution.py:224
  178.2 7.9 %collective-permute-start.49 = (bf16[64,4096]{1,0:T(8,128)(2,1)S(1)}, bf16[64,4096]{1,0:T(8,128)(2,1)S(1)}, u32[]{:S(2)}, u32[]{:S(2)}) collective-permute-start(bf16[64,4096]{1,0:T(8,128)(2,1)S(1)} %constant_dynamic-update-slice_fusion.4.mine), channel_id=1, source_target_pairs={{0,1},{1,0},{2,3},{3,2},{4,5},{5,4},{6,7},{7,6},{8,9},{9,8},{10,11... | collective-permute-start | bytes 1572872 | tf_op jit(solution)/shard_map/head1/ppermute | solution.py:31
  186.1 1.5 collective-permute-done.49.theirs
  187.6 2.4 %head_block.3 = (f32[128,768]{1,0:T(8,128)S(1)}, f32[8,128]{1,0:T(8,128)S(1)}, f32[2,64,64]{2,1,0:T(8,128)S(1)}) custom-call(s32[2]{0:T(128)S(1)} %pad_add_fusion.at_ref, bf16[64,4096]{1,0:T(8,128)(2,1)S(1)} %constant_dynamic-update-slice_fusion.4.mine, bf16[64,4096]{1,0:T(8,128)(2,1)S(1)} %collective-permute-done.49.theirs, ...), custom_call_target="tpu_custom_call" | custom-call | flops 4000000000 | bytes 6291456 | tf_op jit(solution)/shard_map/head1/head_block/pallas_call | solution.py:224
  190.1 14.2 %all_to_all.15 = f32[32,3,256]{2,1,0:T(4,128)S(1)} all-to-all(f32[32,3,256]{2,1,0:T(4,128)S(1)} %broadcast_in_dim.19), channel_id=1, replica_groups=mesh['dp'=8,'pipe'=4,'tensor'=8] {'pipe','tensor'}, dimensions={0} | all-to-all | bytes 196608 | tf_op jit(solution)/shard_map/scores/all_to_all | solution.py:24
  205.8 3.8 %all-to-all-start.2 = ((f32[32,1,4]{2,1,0:T(1,128)}), f32[32,1,4]{2,1,0:T(1,128)S(1)}, u32[]{:S(2)}, u32[]{:S(2)}) async-start(f32[32,1,4]{2,1,0:T(1,128)} %broadcast_in_dim.21), calls=%async_computation.2 | async-start | bytes 32768 | tf_op jit(solution)/shard_map/scores/all_to_all | solution.py:24
  210.3 6.3 %all-to-all-done.2 = f32[32,1,4]{2,1,0:T(1,128)S(1)} async-done(((f32[32,1,4]{2,1,0:T(1,128)}), f32[32,1,4]{2,1,0:T(1,128)S(1)}, u32[]{:S(2)}, u32[]{:S(2)}) %all-to-all-start.2) | async-done | bytes 544 | tf_op jit(solution)/shard_map/scores/all_to_all | solution.py:24
  (121 shorter events, 26.2 us)
Async XLA Ops:
  0.6 18.4 %collective-permute-start.1 = (bf16[4096,256]{1,0:T(8,128)(2,1)}, bf16[4096,256]{1,0:T(8,128)(2,1)S(1)}, u32[]{:S(2)}, u32[]{:S(2)}) collective-permute-start(bf16[4096,256]{1,0:T(8,128)(2,1)} %bitcast.39), channel_id=1, source_target_pairs={{0,1},{1,0},{2,3},{3,2},{4,5},{5,4},{6,7},{7,6},{8,9},{9,8},{10,11... | collective-permute-start | bytes 6291464 | tf_op jit(solution)/shard_map/ppermute | solution.py:31
  3.9 15.2 %collective-permute-start.4 = (bf16[256,4096]{1,0:T(8,128)(2,1)}, bf16[256,4096]{1,0:T(8,128)(2,1)}, u32[]{:S(2)}, u32[]{:S(2)}) collective-permute-start(bf16[256,4096]{1,0:T(8,128)(2,1)} %bitcast.41), channel_id=1, source_target_pairs={{0,1},{1,0},{2,3},{3,2},{4,5},{5,4},{6,7},{7,6},{8,9},{9,8},{10,11... | collective-permute-start | bytes 6291464 | tf_op jit(solution)/shard_map/ppermute | solution.py:31
  5.9 13.2 %all-to-all-start = ((bf16[8,8,4096]{2,1,0:T(8,128)(2,1)}), bf16[8,8,4096]{2,1,0:T(8,128)(2,1)S(1)}, u32[]{:S(2)}, u32[]{:S(2)}) async-start(bf16[8,8,4096]{2,1,0:T(8,128)(2,1)} %bitcast.4), calls=%async_computation | async-start | bytes 1048576 | tf_op jit(solution)/shard_map/all_to_all | solution.py:297
  9.7 9.4 %collective-permute-start.2 = (bf16[4096,128]{1,0:T(8,128)(2,1)}, bf16[4096,128]{1,0:T(8,128)(2,1)}, u32[]{:S(2)}, u32[]{:S(2)}) collective-permute-start(bf16[4096,128]{1,0:T(8,128)(2,1)} %bitcast.43), channel_id=1, source_target_pairs={{0,1},{1,0},{2,3},{3,2},{4,5},{5,4},{6,7},{7,6},{8,9},{9,8},{10,11... | collective-permute-start | bytes 3145736 | tf_op jit(solution)/shard_map/ppermute | solution.py:31
  9.8 9.2 %collective-permute-start.3 = (bf16[4096,128]{1,0:T(8,128)(2,1)}, bf16[4096,128]{1,0:T(8,128)(2,1)}, u32[]{:S(2)}, u32[]{:S(2)}) collective-permute-start(bf16[4096,128]{1,0:T(8,128)(2,1)} %bitcast.45), channel_id=1, source_target_pairs={{0,1},{1,0},{2,3},{3,2},{4,5},{5,4},{6,7},{7,6},{8,9},{9,8},{10,11... | collective-permute-start | bytes 3145736 | tf_op jit(solution)/shard_map/ppermute | solution.py:31
  19.0 6.1 %copy-start = (f32[1,4096]{1,0:T(1,128)S(1)}, f32[1,4096]{1,0:T(1,128)}, u32[]{:S(2)}) copy-start(f32[1,4096]{1,0:T(1,128)} %gain_ref.1) | copy-start | bytes 49156
  19.1 1.3 copy-start.1
  25.1 23.4 %slice-start = ((s8[6291456]{0:T(1024)(128)(4,1)}), s8[4194304]{0:T(1024)(128)(4,1)S(1)}, s32[]{:S(2)}) async-start(s8[6291456]{0:T(1024)(128)(4,1)} %bitcast.31), calls=%async_computation.3 | async-start | bytes 8388608
  25.2 23.4 %slice-start.1 = ((s8[6291456]{0:T(1024)(128)(4,1)}), s8[2097152]{0:T(1024)(128)(4,1)S(1)}, s32[]{:S(2)}) async-start(s8[6291456]{0:T(1024)(128)(4,1)} %bitcast.31), calls=%async_computation.4 | async-start | bytes 4194304
  29.7 3.9 %collective-permute-start.5 = (bf16[16,4096]{1,0:T(8,128)(2,1)S(1)}, bf16[16,4096]{1,0:T(8,128)(2,1)S(1)}, u32[]{:S(2)}, u32[]{:S(2)}) collective-permute-start(bf16[16,4096]{1,0:T(8,128)(2,1)S(1)} %get-tuple-element.120), channel_id=1, source_target_pairs={{0,2},{1,3},{2,0},{3,1},{4,6},{5,7},{6,4},{7,5},{8,10},{9,11},{10,... | collective-permute-start | bytes 393224 | tf_op jit(solution)/shard_map/tick0/ppermute | solution.py:36
  30.0 6.9 %collective-permute-start.6 = (bf16[16,4096]{1,0:T(8,128)(2,1)S(1)}, bf16[16,4096]{1,0:T(8,128)(2,1)S(1)}, u32[]{:S(2)}, u32[]{:S(2)}) collective-permute-start(bf16[16,4096]{1,0:T(8,128)(2,1)S(1)} %get-tuple-element.121), channel_id=1, source_target_pairs={{0,4},{1,5},{2,6},{3,7},{4,0},{5,1},{6,2},{7,3},{8,12},{9,13},{10,... | collective-permute-start | bytes 393224 | tf_op jit(solution)/shard_map/tick0/ppermute | solution.py:36
  31.8 8.0 %collective-permute-start.7 = (bf16[16,4096]{1,0:T(8,128)(2,1)S(1)}, bf16[16,4096]{1,0:T(8,128)(2,1)S(1)}, u32[]{:S(2)}, u32[]{:S(2)}) collective-permute-start(bf16[16,4096]{1,0:T(8,128)(2,1)S(1)} %get-tuple-element.122), channel_id=1, source_target_pairs={{0,6},{1,7},{2,4},{3,5},{4,2},{5,3},{6,0},{7,1},{8,14},{9,15},{10,... | collective-permute-start | bytes 393224 | tf_op jit(solution)/shard_map/tick0/ppermute | solution.py:36
  39.9 5.0 %collective-permute-start.8 = (bf16[16,4096]{1,0:T(8,128)(2,1)S(1)}, bf16[16,4096]{1,0:T(8,128)(2,1)S(1)}, u32[]{:S(2)}, u32[]{:S(2)}) collective-permute-start(bf16[16,4096]{1,0:T(8,128)(2,1)S(1)} %add_convert_fusion.4), channel_id=1, source_target_pairs={{0,8},{8,16},{16,24},{1,9},{9,17},{17,25},{2,10},{10,18},{18,26},{... | collective-permute-start | bytes 393224 | tf_op jit(solution)/shard_map/hop1/ppermute | solution.py:41
  42.4 2.5 %collective-permute-start = (bf16[1,8,4096]{2,1,0:T(8,128)(2,1)S(1)}, bf16[1,8,4096]{2,1,0:T(8,128)(2,1)S(1)}, u32[]{:S(2)}, u32[]{:S(2)}) collective-permute-start(bf16[1,8,4096]{2,1,0:T(8,128)(2,1)S(1)} %get-tuple-element.218), channel_id=1, source_target_pairs={{0,1},{1,0},{2,3},{3,2},{4,5},{5,4},{6,7},{7,6},{8,9},{9,8},{10,11... | collective-permute-start | bytes 196616 | tf_op jit(solution)/shard_map/ppermute | solution.py:31
  45.2 5.1 %collective-permute-start.11 = (bf16[16,4096]{1,0:T(8,128)(2,1)S(1)}, bf16[16,4096]{1,0:T(8,128)(2,1)S(1)}, u32[]{:S(2)}, u32[]{:S(2)}) collective-permute-start(bf16[16,4096]{1,0:T(8,128)(2,1)S(1)} %fusion.2.r0), channel_id=1, source_target_pairs={{0,6},{1,7},{2,4},{3,5},{4,2},{5,3},{6,0},{7,1},{8,14},{9,15},{10,... | collective-permute-start | bytes 393224 | tf_op jit(solution)/shard_map/tick1/ppermute | solution.py:36
  47.1 5.4 %collective-permute-start.10 = (bf16[16,4096]{1,0:T(8,128)(2,1)S(1)}, bf16[16,4096]{1,0:T(8,128)(2,1)S(1)}, u32[]{:S(2)}, u32[]{:S(2)}) collective-permute-start(bf16[16,4096]{1,0:T(8,128)(2,1)S(1)} %fusion.2.r0), channel_id=1, source_target_pairs={{0,4},{1,5},{2,6},{3,7},{4,0},{5,1},{6,2},{7,3},{8,12},{9,13},{10,... | collective-permute-start | bytes 393224 | tf_op jit(solution)/shard_map/tick1/ppermute | solution.py:36
  47.1 6.2 %collective-permute-start.9 = (bf16[16,4096]{1,0:T(8,128)(2,1)S(1)}, bf16[16,4096]{1,0:T(8,128)(2,1)S(1)}, u32[]{:S(2)}, u32[]{:S(2)}) collective-permute-start(bf16[16,4096]{1,0:T(8,128)(2,1)S(1)} %fusion.2.r0), channel_id=1, source_target_pairs={{0,2},{1,3},{2,0},{3,1},{4,6},{5,7},{6,4},{7,5},{8,10},{9,11},{10,... | collective-permute-start | bytes 393224 | tf_op jit(solution)/shard_map/tick1/ppermute | solution.py:36
  57.0 3.9 %collective-permute-start.12 = (bf16[16,4096]{1,0:T(8,128)(2,1)S(1)}, bf16[16,4096]{1,0:T(8,128)(2,1)S(1)}, u32[]{:S(2)}, u32[]{:S(2)}) collective-permute-start(bf16[16,4096]{1,0:T(8,128)(2,1)S(1)} %get-tuple-element.133), channel_id=1, source_target_pairs={{0,2},{1,3},{2,0},{3,1},{4,6},{5,7},{6,4},{7,5},{8,10},{9,11},{10,... | collective-permute-start | bytes 393224 | tf_op jit(solution)/shard_map/tick1/ppermute | solution.py:36
  57.4 6.4 %collective-permute-start.13 = (bf16[16,4096]{1,0:T(8,128)(2,1)S(1)}, bf16[16,4096]{1,0:T(8,128)(2,1)S(1)}, u32[]{:S(2)}, u32[]{:S(2)}) collective-permute-start(bf16[16,4096]{1,0:T(8,128)(2,1)S(1)} %get-tuple-element.134), channel_id=1, source_target_pairs={{0,4},{1,5},{2,6},{3,7},{4,0},{5,1},{6,2},{7,3},{8,12},{9,13},{10,... | collective-permute-start | bytes 393224 | tf_op jit(solution)/shard_map/tick1/ppermute | solution.py:36
  60.0 5.2 %collective-permute-start.14 = (bf16[16,4096]{1,0:T(8,128)(2,1)S(1)}, bf16[16,4096]{1,0:T(8,128)(2,1)S(1)}, u32[]{:S(2)}, u32[]{:S(2)}) collective-permute-start(bf16[16,4096]{1,0:T(8,128)(2,1)S(1)} %get-tuple-element.135), channel_id=1, source_target_pairs={{0,6},{1,7},{2,4},{3,5},{4,2},{5,3},{6,0},{7,1},{8,14},{9,15},{10,... | collective-permute-start | bytes 393224 | tf_op jit(solution)/shard_map/tick1/ppermute | solution.py:36
  65.3 4.4 %collective-permute-start.15 = (bf16[16,4096]{1,0:T(8,128)(2,1)S(1)}, bf16[16,4096]{1,0:T(8,128)(2,1)S(1)}, u32[]{:S(2)}, u32[]{:S(2)}) collective-permute-start(bf16[16,4096]{1,0:T(8,128)(2,1)S(1)} %add_convert_fusion.3), channel_id=1, source_target_pairs={{0,8},{8,16},{16,24},{1,9},{9,17},{17,25},{2,10},{10,18},{18,26},{... | collective-permute-start | bytes 393224 | tf_op jit(solution)/shard_map/hop2/ppermute | solution.py:41
  69.9 5.1 %collective-permute-start.18 = (bf16[16,4096]{1,0:T(8,128)(2,1)S(1)}, bf16[16,4096]{1,0:T(8,128)(2,1)S(1)}, u32[]{:S(2)}, u32[]{:S(2)}) collective-permute-start(bf16[16,4096]{1,0:T(8,128)(2,1)S(1)} %fusion.5.r0), channel_id=1, source_target_pairs={{0,6},{1,7},{2,4},{3,5},{4,2},{5,3},{6,0},{7,1},{8,14},{9,15},{10,... | collective-permute-start | bytes 393224 | tf_op jit(solution)/shard_map/tick2/ppermute | solution.py:36
  71.1 5.4 %collective-permute-start.17 = (bf16[16,4096]{1,0:T(8,128)(2,1)S(1)}, bf16[16,4096]{1,0:T(8,128)(2,1)S(1)}, u32[]{:S(2)}, u32[]{:S(2)}) collective-permute-start(bf16[16,4096]{1,0:T(8,128)(2,1)S(1)} %fusion.5.r0), channel_id=1, source_target_pairs={{0,4},{1,5},{2,6},{3,7},{4,0},{5,1},{6,2},{7,3},{8,12},{9,13},{10,... | collective-permute-start | bytes 393224 | tf_op jit(solution)/shard_map/tick2/ppermute | solution.py:36
  72.2 4.8 %collective-permute-start.16 = (bf16[16,4096]{1,0:T(8,128)(2,1)S(1)}, bf16[16,4096]{1,0:T(8,128)(2,1)S(1)}, u32[]{:S(2)}, u32[]{:S(2)}) collective-permute-start(bf16[16,4096]{1,0:T(8,128)(2,1)S(1)} %fusion.5.r0), channel_id=1, source_target_pairs={{0,2},{1,3},{2,0},{3,1},{4,6},{5,7},{6,4},{7,5},{8,10},{9,11},{10,... | collective-permute-start | bytes 393224 | tf_op jit(solution)/shard_map/tick2/ppermute | solution.py:36
  80.7 4.5 %collective-permute-start.19 = (bf16[16,4096]{1,0:T(8,128)(2,1)S(1)}, bf16[16,4096]{1,0:T(8,128)(2,1)S(1)}, u32[]{:S(2)}, u32[]{:S(2)}) collective-permute-start(bf16[16,4096]{1,0:T(8,128)(2,1)S(1)} %get-tuple-element.144), channel_id=1, source_target_pairs={{0,2},{1,3},{2,0},{3,1},{4,6},{5,7},{6,4},{7,5},{8,10},{9,11},{10,... | collective-permute-start | bytes 393224 | tf_op jit(solution)/shard_map/tick2/ppermute | solution.py:36
  81.2 6.1 %collective-permute-start.20 = (bf16[16,4096]{1,0:T(8,128)(2,1)S(1)}, bf16[16,4096]{1,0:T(8,128)(2,1)S(1)}, u32[]{:S(2)}, u32[]{:S(2)}) collective-permute-start(bf16[16,4096]{1,0:T(8,128)(2,1)S(1)} %get-tuple-element.145), channel_id=1, source_target_pairs={{0,4},{1,5},{2,6},{3,7},{4,0},{5,1},{6,2},{7,3},{8,12},{9,13},{10,... | collective-permute-start | bytes 393224 | tf_op jit(solution)/shard_map/tick2/ppermute | solution.py:36
  83.0 5.6 %collective-permute-start.21 = (bf16[16,4096]{1,0:T(8,128)(2,1)S(1)}, bf16[16,4096]{1,0:T(8,128)(2,1)S(1)}, u32[]{:S(2)}, u32[]{:S(2)}) collective-permute-start(bf16[16,4096]{1,0:T(8,128)(2,1)S(1)} %get-tuple-element.146), channel_id=1, source_target_pairs={{0,6},{1,7},{2,4},{3,5},{4,2},{5,3},{6,0},{7,1},{8,14},{9,15},{10,... | collective-permute-start | bytes 393224 | tf_op jit(solution)/shard_map/tick2/ppermute | solution.py:36
  88.8 6.0 %collective-permute-start.22 = (bf16[16,4096]{1,0:T(8,128)(2,1)S(1)}, bf16[16,4096]{1,0:T(8,128)(2,1)S(1)}, u32[]{:S(2)}, u32[]{:S(2)}) collective-permute-start(bf16[16,4096]{1,0:T(8,128)(2,1)S(1)} %add_convert_fusion.2), channel_id=1, source_target_pairs={{0,8},{8,16},{16,24},{1,9},{9,17},{17,25},{2,10},{10,18},{18,26},{... | collective-permute-start | bytes 393224 | tf_op jit(solution)/shard_map/hop3/ppermute | solution.py:41
  95.0 26.8 %copy-start.2 = (f32[4096]{0:T(1024)S(1)}, f32[4096]{0:T(1024)}, u32[]{:S(2)}) copy-start(f32[4096]{0:T(1024)} %param.16) | copy-start | bytes 49156
  95.0 5.1 %collective-permute-start.25 = (bf16[16,4096]{1,0:T(8,128)(2,1)S(1)}, bf16[16,4096]{1,0:T(8,128)(2,1)S(1)}, u32[]{:S(2)}, u32[]{:S(2)}) collective-permute-start(bf16[16,4096]{1,0:T(8,128)(2,1)S(1)} %fusion.8.r0), channel_id=1, source_target_pairs={{0,6},{1,7},{2,4},{3,5},{4,2},{5,3},{6,0},{7,1},{8,14},{9,15},{10,... | collective-permute-start | bytes 393224 | tf_op jit(solution)/shard_map/tick3/ppermute | solution.py:36
  96.8 5.3 %collective-permute-start.24 = (bf16[16,4096]{1,0:T(8,128)(2,1)S(1)}, bf16[16,4096]{1,0:T(8,128)(2,1)S(1)}, u32[]{:S(2)}, u32[]{:S(2)}) collective-permute-start(bf16[16,4096]{1,0:T(8,128)(2,1)S(1)} %fusion.8.r0), channel_id=1, source_target_pairs={{0,4},{1,5},{2,6},{3,7},{4,0},{5,1},{6,2},{7,3},{8,12},{9,13},{10,... | collective-permute-start | bytes 393224 | tf_op jit(solution)/shard_map/tick3/ppermute | solution.py:36
  96.8 5.4 %collective-permute-start.23 = (bf16[16,4096]{1,0:T(8,128)(2,1)S(1)}, bf16[16,4096]{1,0:T(8,128)(2,1)S(1)}, u32[]{:S(2)}, u32[]{:S(2)}) collective-permute-start(bf16[16,4096]{1,0:T(8,128)(2,1)S(1)} %fusion.8.r0), channel_id=1, source_target_pairs={{0,2},{1,3},{2,0},{3,1},{4,6},{5,7},{6,4},{7,5},{8,10},{9,11},{10,... | collective-permute-start | bytes 393224 | tf_op jit(solution)/shard_map/tick3/ppermute | solution.py:36
  105.9 4.2 %collective-permute-start.26 = (bf16[16,4096]{1,0:T(8,128)(2,1)S(1)}, bf16[16,4096]{1,0:T(8,128)(2,1)S(1)}, u32[]{:S(2)}, u32[]{:S(2)}) collective-permute-start(bf16[16,4096]{1,0:T(8,128)(2,1)S(1)} %get-tuple-element.155), channel_id=1, source_target_pairs={{0,2},{1,3},{2,0},{3,1},{4,6},{5,7},{6,4},{7,5},{8,10},{9,11},{10,... | collective-permute-start | bytes 393224 | tf_op jit(solution)/shard_map/tick3/ppermute | solution.py:36
  106.0 7.8 %collective-permute-start.27 = (bf16[16,4096]{1,0:T(8,128)(2,1)S(1)}, bf16[16,4096]{1,0:T(8,128)(2,1)S(1)}, u32[]{:S(2)}, u32[]{:S(2)}) collective-permute-start(bf16[16,4096]{1,0:T(8,128)(2,1)S(1)} %get-tuple-element.156), channel_id=1, source_target_pairs={{0,4},{1,5},{2,6},{3,7},{4,0},{5,1},{6,2},{7,3},{8,12},{9,13},{10,... | collective-permute-start | bytes 393224 | tf_op jit(solution)/shard_map/tick3/ppermute | solution.py:36
  108.8 6.6 %collective-permute-start.28 = (bf16[16,4096]{1,0:T(8,128)(2,1)S(1)}, bf16[16,4096]{1,0:T(8,128)(2,1)S(1)}, u32[]{:S(2)}, u32[]{:S(2)}) collective-permute-start(bf16[16,4096]{1,0:T(8,128)(2,1)S(1)} %get-tuple-element.157), channel_id=1, source_target_pairs={{0,6},{1,7},{2,4},{3,5},{4,2},{5,3},{6,0},{7,1},{8,14},{9,15},{10,... | collective-permute-start | bytes 393224 | tf_op jit(solution)/shard_map/tick3/ppermute | solution.py:36
  115.4 6.0 %collective-permute-start.29 = (bf16[16,4096]{1,0:T(8,128)(2,1)S(1)}, bf16[16,4096]{1,0:T(8,128)(2,1)S(1)}, u32[]{:S(2)}, u32[]{:S(2)}) collective-permute-start(bf16[16,4096]{1,0:T(8,128)(2,1)S(1)} %add_convert_fusion.1), channel_id=1, source_target_pairs={{0,8},{8,16},{16,24},{1,9},{9,17},{17,25},{2,10},{10,18},{18,26},{... | collective-permute-start | bytes 393224 | tf_op jit(solution)/shard_map/hop4/ppermute | solution.py:41
  122.0 6.9 %collective-permute-start.35 = (bf16[16,4096]{1,0:T(8,128)(2,1)S(1)}, bf16[16,4096]{1,0:T(8,128)(2,1)S(1)}, u32[]{:S(2)}, u32[]{:S(2)}) collective-permute-start(bf16[16,4096]{1,0:T(8,128)(2,1)S(1)} %fusion.14), channel_id=1, source_target_pairs={{24,0},{25,1},{26,2},{27,3},{28,4},{29,5},{30,6},{31,7},{56,32},{5... | collective-permute-start | bytes 393224 | tf_op jit(solution)/shard_map/spread0/ppermute | solution.py:364
  123.3 5.6 %collective-permute-start.34 = (bf16[16,4096]{1,0:T(8,128)(2,1)S(1)}, bf16[16,4096]{1,0:T(8,128)(2,1)S(1)}, u32[]{:S(2)}, u32[]{:S(2)}) collective-permute-start(bf16[16,4096]{1,0:T(8,128)(2,1)S(1)} %fusion.14), channel_id=1, source_target_pairs={{24,8},{25,9},{26,10},{27,11},{28,12},{29,13},{30,14},{31,15},{56,... | collective-permute-start | bytes 393224 | tf_op jit(solution)/shard_map/spread0/ppermute | solution.py:364
  123.9 5.0 %collective-permute-start.33 = (bf16[16,4096]{1,0:T(8,128)(2,1)S(1)}, bf16[16,4096]{1,0:T(8,128)(2,1)S(1)}, u32[]{:S(2)}, u32[]{:S(2)}) collective-permute-start(bf16[16,4096]{1,0:T(8,128)(2,1)S(1)} %fusion.14), channel_id=1, source_target_pairs={{24,16},{25,17},{26,18},{27,19},{28,20},{29,21},{30,22},{31,23},{5... | collective-permute-start | bytes 393224 | tf_op jit(solution)/shard_map/spread0/ppermute | solution.py:364
  124.6 5.1 %collective-permute-start.32 = (bf16[16,4096]{1,0:T(8,128)(2,1)S(1)}, bf16[16,4096]{1,0:T(8,128)(2,1)S(1)}, u32[]{:S(2)}, u32[]{:S(2)}) collective-permute-start(bf16[16,4096]{1,0:T(8,128)(2,1)S(1)} %fusion.11.r0), channel_id=1, source_target_pairs={{0,6},{1,7},{2,4},{3,5},{4,2},{5,3},{6,0},{7,1},{8,14},{9,15},{10,... | collective-permute-start | bytes 393224 | tf_op jit(solution)/shard_map/tick4/ppermute | solution.py:36
  126.0 5.3 %collective-permute-start.31 = (bf16[16,4096]{1,0:T(8,128)(2,1)S(1)}, bf16[16,4096]{1,0:T(8,128)(2,1)S(1)}, u32[]{:S(2)}, u32[]{:S(2)}) collective-permute-start(bf16[16,4096]{1,0:T(8,128)(2,1)S(1)} %fusion.11.r0), channel_id=1, source_target_pairs={{0,4},{1,5},{2,6},{3,7},{4,0},{5,1},{6,2},{7,3},{8,12},{9,13},{10,... | collective-permute-start | bytes 393224 | tf_op jit(solution)/shard_map/tick4/ppermute | solution.py:36
  128.9 3.8 %collective-permute-start.30 = (bf16[16,4096]{1,0:T(8,128)(2,1)S(1)}, bf16[16,4096]{1,0:T(8,128)(2,1)S(1)}, u32[]{:S(2)}, u32[]{:S(2)}) collective-permute-start(bf16[16,4096]{1,0:T(8,128)(2,1)S(1)} %fusion.11.r0), channel_id=1, source_target_pairs={{0,2},{1,3},{2,0},{3,1},{4,6},{5,7},{6,4},{7,5},{8,10},{9,11},{10,... | collective-permute-start | bytes 393224 | tf_op jit(solution)/shard_map/tick4/ppermute | solution.py:36
  136.4 5.3 %collective-permute-start.36 = (bf16[16,4096]{1,0:T(8,128)(2,1)S(1)}, bf16[16,4096]{1,0:T(8,128)(2,1)S(1)}, u32[]{:S(2)}, u32[]{:S(2)}) collective-permute-start(bf16[16,4096]{1,0:T(8,128)(2,1)S(1)} %get-tuple-element.169), channel_id=1, source_target_pairs={{0,2},{1,3},{2,0},{3,1},{4,6},{5,7},{6,4},{7,5},{8,10},{9,11},{10,... | collective-permute-start | bytes 393224 | tf_op jit(solution)/shard_map/tick4/ppermute | solution.py:36
  136.5 7.1 %collective-permute-start.37 = (bf16[16,4096]{1,0:T(8,128)(2,1)S(1)}, bf16[16,4096]{1,0:T(8,128)(2,1)S(1)}, u32[]{:S(2)}, u32[]{:S(2)}) collective-permute-start(bf16[16,4096]{1,0:T(8,128)(2,1)S(1)} %get-tuple-element.170), channel_id=1, source_target_pairs={{0,4},{1,5},{2,6},{3,7},{4,0},{5,1},{6,2},{7,3},{8,12},{9,13},{10,... | collective-permute-start | bytes 393224 | tf_op jit(solution)/shard_map/tick4/ppermute | solution.py:36
  139.0 9.6 %collective-permute-start.38 = (bf16[16,4096]{1,0:T(8,128)(2,1)S(1)}, bf16[16,4096]{1,0:T(8,128)(2,1)S(1)}, u32[]{:S(2)}, u32[]{:S(2)}) collective-permute-start(bf16[16,4096]{1,0:T(8,128)(2,1)S(1)} %get-tuple-element.171), channel_id=1, source_target_pairs={{0,6},{1,7},{2,4},{3,5},{4,2},{5,3},{6,0},{7,1},{8,14},{9,15},{10,... | collective-permute-start | bytes 393224 | tf_op jit(solution)/shard_map/tick4/ppermute | solution.py:36
  140.3 9.4 %collective-permute-start.41 = (bf16[16,4096]{1,0:T(8,128)(2,1)S(1)}, bf16[16,4096]{1,0:T(8,128)(2,1)S(1)}, u32[]{:S(2)}, u32[]{:S(2)}) collective-permute-start(bf16[16,4096]{1,0:T(8,128)(2,1)S(1)} %select_select_fusion.1), channel_id=1, source_target_pairs={{0,6},{1,7},{2,4},{3,5},{4,2},{5,3},{6,0},{7,1},{8,14},{9,15},{10,... | collective-permute-start | bytes 393224 | tf_op jit(solution)/shard_map/tick4/ppermute | solution.py:36
  141.7 8.1 %collective-permute-start.40 = (bf16[16,4096]{1,0:T(8,128)(2,1)S(1)}, bf16[16,4096]{1,0:T(8,128)(2,1)S(1)}, u32[]{:S(2)}, u32[]{:S(2)}) collective-permute-start(bf16[16,4096]{1,0:T(8,128)(2,1)S(1)} %select_select_fusion.1), channel_id=1, source_target_pairs={{0,4},{1,5},{2,6},{3,7},{4,0},{5,1},{6,2},{7,3},{8,12},{9,13},{10,... | collective-permute-start | bytes 393224 | tf_op jit(solution)/shard_map/tick4/ppermute | solution.py:36
  141.7 8.1 %collective-permute-start.39 = (bf16[16,4096]{1,0:T(8,128)(2,1)S(1)}, bf16[16,4096]{1,0:T(8,128)(2,1)S(1)}, u32[]{:S(2)}, u32[]{:S(2)}) collective-permute-start(bf16[16,4096]{1,0:T(8,128)(2,1)S(1)} %select_select_fusion.1), channel_id=1, source_target_pairs={{0,2},{1,3},{2,0},{3,1},{4,6},{5,7},{6,4},{7,5},{8,10},{9,11},{10,... | collective-permute-start | bytes 393224 | tf_op jit(solution)/shard_map/tick4/ppermute | solution.py:36
  150.1 19.5 %collective-permute-start.44 = (bf16[16,4096]{1,0:T(8,128)(2,1)S(1)}, bf16[16,4096]{1,0:T(8,128)(2,1)S(1)}, u32[]{:S(2)}, u32[]{:S(2)}) collective-permute-start(bf16[16,4096]{1,0:T(8,128)(2,1)S(1)} %fusion.17), channel_id=1, source_target_pairs={{24,0},{25,1},{26,2},{27,3},{28,4},{29,5},{30,6},{31,7},{56,32},{5... | collective-permute-start | bytes 393224 | tf_op jit(solution)/shard_map/spread1/ppermute | solution.py:364
  151.4 18.2 %collective-permute-start.43 = (bf16[16,4096]{1,0:T(8,128)(2,1)S(1)}, bf16[16,4096]{1,0:T(8,128)(2,1)S(1)}, u32[]{:S(2)}, u32[]{:S(2)}) collective-permute-start(bf16[16,4096]{1,0:T(8,128)(2,1)S(1)} %fusion.17), channel_id=1, source_target_pairs={{24,8},{25,9},{26,10},{27,11},{28,12},{29,13},{30,14},{31,15},{56,... | collective-permute-start | bytes 393224 | tf_op jit(solution)/shard_map/spread1/ppermute | solution.py:364
  152.1 17.5 %collective-permute-start.42 = (bf16[16,4096]{1,0:T(8,128)(2,1)S(1)}, bf16[16,4096]{1,0:T(8,128)(2,1)S(1)}, u32[]{:S(2)}, u32[]{:S(2)}) collective-permute-start(bf16[16,4096]{1,0:T(8,128)(2,1)S(1)} %fusion.17), channel_id=1, source_target_pairs={{24,16},{25,17},{26,18},{27,19},{28,20},{29,21},{30,22},{31,23},{5... | collective-permute-start | bytes 393224 | tf_op jit(solution)/shard_map/spread1/ppermute | solution.py:364
  152.8 18.3 %collective-permute-start.45 = (bf16[64,4096]{1,0:T(8,128)(2,1)S(1)}, bf16[64,4096]{1,0:T(8,128)(2,1)S(1)}, u32[]{:S(2)}, u32[]{:S(2)}) collective-permute-start(bf16[64,4096]{1,0:T(8,128)(2,1)S(1)} %constant_dynamic-update-slice_fusion.mine), channel_id=1, source_target_pairs={{0,1},{1,0},{2,3},{3,2},{4,5},{5,4},{6,7},{7,6},{8,9},{9,8},{10,11... | collective-permute-start | bytes 1572872 | tf_op jit(solution)/shard_map/head0/ppermute | solution.py:31
  171.1 5.7 %collective-permute-start.48 = (bf16[16,4096]{1,0:T(8,128)(2,1)S(1)}, bf16[16,4096]{1,0:T(8,128)(2,1)S(1)}, u32[]{:S(2)}, u32[]{:S(2)}) collective-permute-start(bf16[16,4096]{1,0:T(8,128)(2,1)S(1)} %select_select_fusion), channel_id=1, source_target_pairs={{0,6},{1,7},{2,4},{3,5},{4,2},{5,3},{6,0},{7,1},{8,14},{9,15},{10,... | collective-permute-start | bytes 393224 | tf_op jit(solution)/shard_map/head1/ppermute | solution.py:36
  172.3 5.3 %collective-permute-start.47 = (bf16[16,4096]{1,0:T(8,128)(2,1)S(1)}, bf16[16,4096]{1,0:T(8,128)(2,1)S(1)}, u32[]{:S(2)}, u32[]{:S(2)}) collective-permute-start(bf16[16,4096]{1,0:T(8,128)(2,1)S(1)} %select_select_fusion), channel_id=1, source_target_pairs={{0,4},{1,5},{2,6},{3,7},{4,0},{5,1},{6,2},{7,3},{8,12},{9,13},{10,... | collective-permute-start | bytes 393224 | tf_op jit(solution)/shard_map/head1/ppermute | solution.py:36
  173.2 4.9 %collective-permute-start.46 = (bf16[16,4096]{1,0:T(8,128)(2,1)S(1)}, bf16[16,4096]{1,0:T(8,128)(2,1)S(1)}, u32[]{:S(2)}, u32[]{:S(2)}) collective-permute-start(bf16[16,4096]{1,0:T(8,128)(2,1)S(1)} %select_select_fusion), channel_id=1, source_target_pairs={{0,2},{1,3},{2,0},{3,1},{4,6},{5,7},{6,4},{7,5},{8,10},{9,11},{10,... | collective-permute-start | bytes 393224 | tf_op jit(solution)/shard_map/head1/ppermute | solution.py:36
  178.2 9.4 %collective-permute-start.49 = (bf16[64,4096]{1,0:T(8,128)(2,1)S(1)}, bf16[64,4096]{1,0:T(8,128)(2,1)S(1)}, u32[]{:S(2)}, u32[]{:S(2)}) collective-permute-start(bf16[64,4096]{1,0:T(8,128)(2,1)S(1)} %constant_dynamic-update-slice_fusion.4.mine), channel_id=1, source_target_pairs={{0,1},{1,0},{2,3},{3,2},{4,5},{5,4},{6,7},{7,6},{8,9},{9,8},{10,11... | collective-permute-start | bytes 1572872 | tf_op jit(solution)/shard_map/head1/ppermute | solution.py:31
  205.8 10.9 %all-to-all-start.2 = ((f32[32,1,4]{2,1,0:T(1,128)}), f32[32,1,4]{2,1,0:T(1,128)S(1)}, u32[]{:S(2)}, u32[]{:S(2)}) async-start(f32[32,1,4]{2,1,0:T(1,128)} %broadcast_in_dim.21), calls=%async_computation.2 | async-start | bytes 32768 | tf_op jit(solution)/shard_map/scores/all_to_all | solution.py:24
where the time goes:
time: 218 us; the launch traced here: 217 us
  starting transfers between devices  94.1 us (43%)
  waiting for transfers between devices  68.9 us (32%)
  Pallas kernels  29.8 us (14%)
  blocking collectives  14.2 us (7%)
  local copies, waits for them, and re-layouts  4.86 us (2%)
  other arithmetic  4.17 us (2%)
    ppermute x33, waiting for transfers between devices, chip_swap(): lax.ppermute(value, 'tensor', [(t, t ^ CORES * k) for t in range(size)])  43 us
    ppermute x33, starting transfers between devices, chip_swap(): lax.ppermute(value, 'tensor', [(t, t ^ CORES * k) for t in range(size)])  38 us
    ppermute x7, starting transfers between devices, core_swap(): return lax.ppermute(value, 'tensor', [(t, t ^ 1) for t in range(size)])  30.2 us
    pallas_call x5, Pallas kernels, section_block(): pl.pallas_call(kernel, out_shape=shapes, in_specs=specs + [IN_VMEM] * 5,...  19.2 us
    all_to_all x1, blocking collectives, sent_to_all(): lax.all_to_all(jnp.broadcast_to(value[None], (size, *value.shape)), axis,...  14.2 us
    ppermute x4, starting transfers between devices, hop(): return lax.ppermute(value, 'pipe', [(i, i + 1) for i in range(size - 1)])  13.1 us
    all_to_all x1, waiting for transfers between devices, per_device(): lax.all_to_all(first_rows, 'tensor', 0, 0, tiled=True)  7.46 us
    all_to_all x1, waiting for transfers between devices, sent_to_all(): lax.all_to_all(jnp.broadcast_to(value[None], (size, *value.shape)), axis,...  6.34 us
  transfers between devices with their start and end apart: 52, of which 34 were waited for; matrix products, arithmetic and copies ran while one was open for 2% of the time, Pallas kernels for 1%

commit v1 on v0

--- a/solution.py
+++ b/solution.py
@@ -85,7 +85,7 @@
     )(*flat)
 
 
-def section_body(rows, context, state, w_in, w_out, cos_ref, sin_ref, bias_ref, outs):
+def section_body(rows, context, state, w_in, w_out, cos_ref, sin_ref, bias_ref, outs, unrolled=False):
     cosine, sine, bias = cos_ref[...], sin_ref[...], bias_ref[...]
     n_rows = rows.shape[0]
     sides, depth, _ = w_out.shape
@@ -117,8 +117,7 @@
     block, width = outs[0].shape
     step = width // 2
 
-    def columns(c, carry):
-        cols = pl.ds(pl.multiple_of(c * step, step), step)
+    def columns(cols):
         part = sum(
             jnp.dot(context[i], w_out[i, :, cols], preferred_element_type=F32)
             for i in range(sides)
@@ -126,9 +125,17 @@
         outs[0][:, cols] = part[:block] + state[:, cols].astype(F32)
         for i in range(1, len(outs)):
             outs[i][:, cols] = part[i * block : (i + 1) * block].astype(BF16)
+
+    if unrolled:
+        for n in range(0, width, 512):
+            columns(slice(n, n + 512))
+        return
+
+    def looped(c, carry):
+        columns(pl.ds(pl.multiple_of(c * step, step), step))
         return carry
 
-    lax.fori_loop(0, width // step, columns, 0)
+    lax.fori_loop(0, width // step, looped, 0)
 
 
 def section_kernel(r0, r1, r2, r3, state, *rest):
@@ -136,7 +143,7 @@
     block = r0.shape[0]
     for i, r in enumerate((r0, r1, r2, r3)):
         rows[i * block : (i + 1) * block, :] = r[...]
-    section_body(rows, context, state, *rest[:5], rest[5:])
+    section_body(rows, context, state, *rest[:5], rest[5:], unrolled=True)
 
 
 def first_kernel(at_ref, whole, gain_ref, *rest):

time: 218 us -> 217 us (level)
  no operation moved by 1% of the time
where the time goes in v1:
time: 217 us
  starting transfers between devices  94 us (43%)
  waiting for transfers between devices  69.2 us (32%)
  Pallas kernels  29.4 us (14%)
  blocking collectives  14.2 us (7%)
  local copies, waits for them, and re-layouts  4.86 us (2%)
  other arithmetic  4.17 us (2%)
    ppermute x33, waiting for transfers between devices, chip_swap(): lax.ppermute(value, 'tensor', [(t, t ^ CORES * k) for t in range(size)])  43.2 us
    ppermute x33, starting transfers between devices, chip_swap(): lax.ppermute(value, 'tensor', [(t, t ^ CORES * k) for t in range(size)])  38.2 us
    ppermute x7, starting transfers between devices, core_swap(): return lax.ppermute(value, 'tensor', [(t, t ^ 1) for t in range(size)])  29.9 us
    pallas_call x5, Pallas kernels, section_block(): pl.pallas_call(kernel, out_shape=shapes, in_specs=specs + [IN_VMEM] * 5,...  18.7 us
    all_to_all x1, blocking collectives, sent_to_all(): lax.all_to_all(jnp.broadcast_to(value[None], (size, *value.shape)), axis,...  14.2 us
    ppermute x4, starting transfers between devices, hop(): return lax.ppermute(value, 'pipe', [(i, i + 1) for i in range(size - 1)])  13.1 us
    all_to_all x1, waiting for transfers between devices, per_device(): lax.all_to_all(first_rows, 'tensor', 0, 0, tiled=True)  7.46 us
    all_to_all x1, waiting for transfers between devices, sent_to_all(): lax.all_to_all(jnp.broadcast_to(value[None], (size, *value.shape)), axis,...  6.34 us
  transfers between devices with their start and end apart: 52, of which 34 were waited for; matrix products, arithmetic and copies ran while one was open for 2% of the time, Pallas kernels for 1%

profile of v1, /device:TPU:1, one launch (start us, length us, event | category | flops | bytes accessed | tf_op | source)
XLA Modules:
  0.0 216.9 jit_solution(3081992709929315330)
XLA Ops:
  0.6 3.3 %collective-permute-start.1 = (bf16[4096,256]{1,0:T(8,128)(2,1)}, bf16[4096,256]{1,0:T(8,128)(2,1)S(1)}, u32[]{:S(2)}, u32[]{:S(2)}) collective-permute-start(bf16[4096,256]{1,0:T(8,128)(2,1)} %bitcast.39), channel_id=1, source_target_pairs={{0,1},{1,0},{2,3},{3,2},{4,5},{5,4},{6,7},{7,6},{8,9},{9,8},{10,11... | collective-permute-start | bytes 6291464 | tf_op jit(solution)/shard_map/ppermute | solution.py:31
  5.9 3.8 %all-to-all-start = ((bf16[8,8,4096]{2,1,0:T(8,128)(2,1)}), bf16[8,8,4096]{2,1,0:T(8,128)(2,1)S(1)}, u32[]{:S(2)}, u32[]{:S(2)}) async-start(bf16[8,8,4096]{2,1,0:T(8,128)(2,1)} %bitcast.4), calls=%async_computation | async-start | bytes 1048576 | tf_op jit(solution)/shard_map/all_to_all | solution.py:304
  11.6 7.5 %all-to-all-done = bf16[8,8,4096]{2,1,0:T(8,128)(2,1)S(1)} async-done(((bf16[8,8,4096]{2,1,0:T(8,128)(2,1)}), bf16[8,8,4096]{2,1,0:T(8,128)(2,1)S(1)}, u32[]{:S(2)}, u32[]{:S(2)}) %all-to-all-start) | async-done | bytes 524320 | tf_op jit(solution)/shard_map/all_to_all | solution.py:304
  19.1 1.3 copy-done.1
  20.4 4.7 %resident.2 = (bf16[2,4096,512]{2,1,0:T(8,128)(2,1)S(1)}, bf16[2,256,4096]{2,1,0:T(8,128)(2,1)S(1)}) custom-call(bf16[4096,256]{1,0:T(8,128)(2,1)} %bitcast.40, bf16[4096,128]{1,0:T(8,128)(2,1)} %bitcast.44, bf16[4096,128]{1,0:T(8,128)(2,1)} %bitcast.46, bf16[4096,256]{1,0:T(8,128)(2,1)} %copy-done.1, bf16[4096,128]{1,0:T(8,128)(2,1)} %collective-permute-done.2.refs_4_, ...), custom_call_target="tpu_custom_call" | custom-call | flops 1000000000 | bytes 25165824 | tf_op jit(solution)/shard_map/resident/pallas_call | solution.py:74
  25.2 4.5 %section_block.5 = (f32[16,4096]{1,0:T(8,128)S(1)}, bf16[16,4096]{1,0:T(8,128)(2,1)S(1)}, bf16[16,4096]{1,0:T(8,128)(2,1)S(1)}, bf16[16,4096]{1,0:T(8,128)(2,1)S(1)}) custom-call(s32[2]{0:T(128)S(1)} %pad_add_fusion.at_ref, bf16[64,4096]{1,0:T(8,128)(2,1)S(1)} %bitcast.33, f32[1,4096]{1,0:T(1,128)S(1)} %copy-done, ...), custom_call_target="tpu_custom_call" | custom-call | flops 8000000000 | bytes 12582912 | tf_op jit(solution)/shard_map/tick0/section_block/pallas_call | solution.py:171
  30.0 1.8 collective-permute-start.6
  31.8 1.8 collective-permute-start.7
  33.6 3.3 %collective-permute-done.6 = bf16[16,4096]{1,0:T(8,128)(2,1)S(1)} collective-permute-done((bf16[16,4096]{1,0:T(8,128)(2,1)S(1)}, bf16[16,4096]{1,0:T(8,128)(2,1)S(1)}, u32[]{:S(2)}, u32[]{:S(2)}) %collective-permute-start.6) | collective-permute-done | bytes 131104 | tf_op jit(solution)/shard_map/tick0/ppermute | solution.py:36
  36.9 2.9 %collective-permute-done.7 = bf16[16,4096]{1,0:T(8,128)(2,1)S(1)} collective-permute-done((bf16[16,4096]{1,0:T(8,128)(2,1)S(1)}, bf16[16,4096]{1,0:T(8,128)(2,1)S(1)}, u32[]{:S(2)}, u32[]{:S(2)}) %collective-permute-start.7) | collective-permute-done | bytes 131104 | tf_op jit(solution)/shard_map/tick0/ppermute | solution.py:36
  39.9 2.5 %collective-permute-start.8 = (bf16[16,4096]{1,0:T(8,128)(2,1)S(1)}, bf16[16,4096]{1,0:T(8,128)(2,1)S(1)}, u32[]{:S(2)}, u32[]{:S(2)}) collective-permute-start(bf16[16,4096]{1,0:T(8,128)(2,1)S(1)} %add_convert_fusion.4), channel_id=1, source_target_pairs={{0,8},{8,16},{16,24},{1,9},{9,17},{17,25},{2,10},{10,18},{18,26},{... | collective-permute-start | bytes 393224 | tf_op jit(solution)/shard_map/hop1/ppermute | solution.py:41
  42.4 1.6 collective-permute-start
  45.2 1.9 collective-permute-start.11
  47.1 1.5 collective-permute-start.9
  49.0 1.3 collective-permute-done.11.r3
  50.3 2.2 %collective-permute-done.10.r2 = bf16[16,4096]{1,0:T(8,128)(2,1)S(1)} collective-permute-done((bf16[16,4096]{1,0:T(8,128)(2,1)S(1)}, bf16[16,4096]{1,0:T(8,128)(2,1)S(1)}, u32[]{:S(2)}, u32[]{:S(2)}) %collective-permute-start.10) | collective-permute-done | bytes 131104 | tf_op jit(solution)/shard_map/tick1/ppermute | solution.py:36
  53.3 3.6 %section_block.6 = (f32[16,4096]{1,0:T(8,128)S(1)}, bf16[16,4096]{1,0:T(8,128)(2,1)S(1)}, bf16[16,4096]{1,0:T(8,128)(2,1)S(1)}, bf16[16,4096]{1,0:T(8,128)(2,1)S(1)}) custom-call(bf16[16,4096]{1,0:T(8,128)(2,1)S(1)} %fusion.2.r0, bf16[16,4096]{1,0:T(8,128)(2,1)S(1)} %collective-permute-done.9.r1, bf16[16,4096]{1,0:T(8,128)(2,1)S(1)} %collective-permute-done.10.r2, ...), custom_call_target="tpu_custom_call" | custom-call | flops 8000000000 | bytes 12582912 | tf_op jit(solution)/shard_map/tick1/section_block/pallas_call | solution.py:171
  57.3 2.7 %collective-permute-start.13 = (bf16[16,4096]{1,0:T(8,128)(2,1)S(1)}, bf16[16,4096]{1,0:T(8,128)(2,1)S(1)}, u32[]{:S(2)}, u32[]{:S(2)}) collective-permute-start(bf16[16,4096]{1,0:T(8,128)(2,1)S(1)} %get-tuple-element.134), channel_id=1, source_target_pairs={{0,4},{1,5},{2,6},{3,7},{4,0},{5,1},{6,2},{7,3},{8,12},{9,13},{10,... | collective-permute-start | bytes 393224 | tf_op jit(solution)/shard_map/tick1/ppermute | solution.py:36
  60.8 2.9 %collective-permute-done.13 = bf16[16,4096]{1,0:T(8,128)(2,1)S(1)} collective-permute-done((bf16[16,4096]{1,0:T(8,128)(2,1)S(1)}, bf16[16,4096]{1,0:T(8,128)(2,1)S(1)}, u32[]{:S(2)}, u32[]{:S(2)}) %collective-permute-start.13) | collective-permute-done | bytes 131104 | tf_op jit(solution)/shard_map/tick1/ppermute | solution.py:36
  63.7 1.4 collective-permute-done.14
  65.2 2.5 %collective-permute-start.15 = (bf16[16,4096]{1,0:T(8,128)(2,1)S(1)}, bf16[16,4096]{1,0:T(8,128)(2,1)S(1)}, u32[]{:S(2)}, u32[]{:S(2)}) collective-permute-start(bf16[16,4096]{1,0:T(8,128)(2,1)S(1)} %add_convert_fusion.3), channel_id=1, source_target_pairs={{0,8},{8,16},{16,24},{1,9},{9,17},{17,25},{2,10},{10,18},{18,26},{... | collective-permute-start | bytes 393224 | tf_op jit(solution)/shard_map/hop2/ppermute | solution.py:41
  67.6 1.9 collective-permute-done.15.state
  73.2 1.8 collective-permute-done.18.r3
  74.9 1.4 collective-permute-done.17.r2
  76.9 3.6 %section_block.7 = (f32[16,4096]{1,0:T(8,128)S(1)}, bf16[16,4096]{1,0:T(8,128)(2,1)S(1)}, bf16[16,4096]{1,0:T(8,128)(2,1)S(1)}, bf16[16,4096]{1,0:T(8,128)(2,1)S(1)}) custom-call(bf16[16,4096]{1,0:T(8,128)(2,1)S(1)} %fusion.5.r0, bf16[16,4096]{1,0:T(8,128)(2,1)S(1)} %collective-permute-done.16.r1, bf16[16,4096]{1,0:T(8,128)(2,1)S(1)} %collective-permute-done.17.r2, ...), custom_call_target="tpu_custom_call" | custom-call | flops 8000000000 | bytes 12582912 | tf_op jit(solution)/shard_map/tick2/section_block/pallas_call | solution.py:171
  81.0 1.8 collective-permute-start.20
  82.8 1.6 collective-permute-start.21
  85.0 2.2 %collective-permute-done.20 = bf16[16,4096]{1,0:T(8,128)(2,1)S(1)} collective-permute-done((bf16[16,4096]{1,0:T(8,128)(2,1)S(1)}, bf16[16,4096]{1,0:T(8,128)(2,1)S(1)}, u32[]{:S(2)}, u32[]{:S(2)}) %collective-permute-start.20) | collective-permute-done | bytes 131104 | tf_op jit(solution)/shard_map/tick2/ppermute | solution.py:36
  87.2 1.3 collective-permute-done.21
  88.6 4.1 %collective-permute-start.22 = (bf16[16,4096]{1,0:T(8,128)(2,1)S(1)}, bf16[16,4096]{1,0:T(8,128)(2,1)S(1)}, u32[]{:S(2)}, u32[]{:S(2)}) collective-permute-start(bf16[16,4096]{1,0:T(8,128)(2,1)S(1)} %add_convert_fusion.2), channel_id=1, source_target_pairs={{0,8},{8,16},{16,24},{1,9},{9,17},{17,25},{2,10},{10,18},{18,26},{... | collective-permute-start | bytes 393224 | tf_op jit(solution)/shard_map/hop3/ppermute | solution.py:41
  92.7 1.9 collective-permute-done.22.state
  94.9 1.8 collective-permute-start.25
  96.7 1.6 collective-permute-start.23
  98.3 1.8 collective-permute-done.25.r3
  100.0 2.0 collective-permute-done.24.r2
  102.1 3.6 %section_block.8 = (f32[16,4096]{1,0:T(8,128)S(1)}, bf16[16,4096]{1,0:T(8,128)(2,1)S(1)}, bf16[16,4096]{1,0:T(8,128)(2,1)S(1)}, bf16[16,4096]{1,0:T(8,128)(2,1)S(1)}) custom-call(bf16[16,4096]{1,0:T(8,128)(2,1)S(1)} %fusion.8.r0, bf16[16,4096]{1,0:T(8,128)(2,1)S(1)} %collective-permute-done.23.r1, bf16[16,4096]{1,0:T(8,128)(2,1)S(1)} %collective-permute-done.24.r2, ...), custom_call_target="tpu_custom_call" | custom-call | flops 8000000000 | bytes 12582912 | tf_op jit(solution)/shard_map/tick3/section_block/pallas_call | solution.py:171
  105.7 2.8 %collective-permute-start.27 = (bf16[16,4096]{1,0:T(8,128)(2,1)S(1)}, bf16[16,4096]{1,0:T(8,128)(2,1)S(1)}, u32[]{:S(2)}, u32[]{:S(2)}) collective-permute-start(bf16[16,4096]{1,0:T(8,128)(2,1)S(1)} %get-tuple-element.156), channel_id=1, source_target_pairs={{0,4},{1,5},{2,6},{3,7},{4,0},{5,1},{6,2},{7,3},{8,12},{9,13},{10,... | collective-permute-start | bytes 393224 | tf_op jit(solution)/shard_map/tick3/ppermute | solution.py:36
  109.8 3.5 %collective-permute-done.27 = bf16[16,4096]{1,0:T(8,128)(2,1)S(1)} collective-permute-done((bf16[16,4096]{1,0:T(8,128)(2,1)S(1)}, bf16[16,4096]{1,0:T(8,128)(2,1)S(1)}, u32[]{:S(2)}, u32[]{:S(2)}) %collective-permute-start.27) | collective-permute-done | bytes 131104 | tf_op jit(solution)/shard_map/tick3/ppermute | solution.py:36
  113.4 1.7 collective-permute-done.28
  115.2 4.1 %collective-permute-start.29 = (bf16[16,4096]{1,0:T(8,128)(2,1)S(1)}, bf16[16,4096]{1,0:T(8,128)(2,1)S(1)}, u32[]{:S(2)}, u32[]{:S(2)}) collective-permute-start(bf16[16,4096]{1,0:T(8,128)(2,1)S(1)} %add_convert_fusion.1), channel_id=1, source_target_pairs={{0,8},{8,16},{16,24},{1,9},{9,17},{17,25},{2,10},{10,18},{18,26},{... | collective-permute-start | bytes 393224 | tf_op jit(solution)/shard_map/hop4/ppermute | solution.py:41
  119.3 1.9 collective-permute-done.29.state
  121.7 1.3 collective-permute-start.35
  124.4 1.5 collective-permute-start.32
  126.1 2.5 %collective-permute-done.35 = bf16[16,4096]{1,0:T(8,128)(2,1)S(1)} collective-permute-done((bf16[16,4096]{1,0:T(8,128)(2,1)S(1)}, bf16[16,4096]{1,0:T(8,128)(2,1)S(1)}, u32[]{:S(2)}, u32[]{:S(2)}) %collective-permute-start.35) | collective-permute-done | bytes 131104 | tf_op jit(solution)/shard_map/spread0/ppermute | solution.py:371
  129.5 1.7 collective-permute-done.31.r2
  131.2 1.2 collective-permute-done.30.r1
  132.5 3.6 %section_block.9 = (f32[16,4096]{1,0:T(8,128)S(1)}, bf16[16,4096]{1,0:T(8,128)(2,1)S(1)}, bf16[16,4096]{1,0:T(8,128)(2,1)S(1)}, bf16[16,4096]{1,0:T(8,128)(2,1)S(1)}) custom-call(bf16[16,4096]{1,0:T(8,128)(2,1)S(1)} %fusion.11.r0, bf16[16,4096]{1,0:T(8,128)(2,1)S(1)} %collective-permute-done.30.r1, bf16[16,4096]{1,0:T(8,128)(2,1)S(1)} %collective-permute-done.31.r2, ...), custom_call_target="tpu_custom_call" | custom-call | flops 8000000000 | bytes 12582912 | tf_op jit(solution)/shard_map/tick4/section_block/pallas_call | solution.py:171
  136.3 2.6 %collective-permute-start.37 = (bf16[16,4096]{1,0:T(8,128)(2,1)S(1)}, bf16[16,4096]{1,0:T(8,128)(2,1)S(1)}, u32[]{:S(2)}, u32[]{:S(2)}) collective-permute-start(bf16[16,4096]{1,0:T(8,128)(2,1)S(1)} %get-tuple-element.170), channel_id=1, source_target_pairs={{0,4},{1,5},{2,6},{3,7},{4,0},{5,1},{6,2},{7,3},{8,12},{9,13},{10,... | collective-permute-start | bytes 393224 | tf_op jit(solution)/shard_map/tick4/ppermute | solution.py:36
  139.0 1.2 collective-permute-start.38
  140.2 1.4 collective-permute-start.41
  141.6 1.8 collective-permute-start.39
  143.4 5.1 %collective-permute-done.38 = bf16[16,4096]{1,0:T(8,128)(2,1)S(1)} collective-permute-done((bf16[16,4096]{1,0:T(8,128)(2,1)S(1)}, bf16[16,4096]{1,0:T(8,128)(2,1)S(1)}, u32[]{:S(2)}, u32[]{:S(2)}) %collective-permute-start.38) | collective-permute-done | bytes 131104 | tf_op jit(solution)/shard_map/tick4/ppermute | solution.py:36
  148.6 1.2 collective-permute-done.41
  150.1 1.3 collective-permute-start.44
  152.8 16.7 %collective-permute-start.45 = (bf16[64,4096]{1,0:T(8,128)(2,1)S(1)}, bf16[64,4096]{1,0:T(8,128)(2,1)S(1)}, u32[]{:S(2)}, u32[]{:S(2)}) collective-permute-start(bf16[64,4096]{1,0:T(8,128)(2,1)S(1)} %constant_dynamic-update-slice_fusion.mine), channel_id=1, source_target_pairs={{0,1},{1,0},{2,3},{3,2},{4,5},{5,4},{6,7},{7,6},{8,9},{9,8},{10,11... | collective-permute-start | bytes 1572872 | tf_op jit(solution)/shard_map/head0/ppermute | solution.py:31
  169.6 1.4 collective-permute-done.45.theirs
  171.0 1.4 collective-permute-start.48
  174.2 2.4 %head_block.2 = (f32[128,768]{1,0:T(8,128)S(1)}, f32[8,128]{1,0:T(8,128)S(1)}, f32[2,64,64]{2,1,0:T(8,128)S(1)}) custom-call(s32[2]{0:T(128)S(1)} %pad_add_fusion.at_ref, bf16[64,4096]{1,0:T(8,128)(2,1)S(1)} %constant_dynamic-update-slice_fusion.mine, bf16[64,4096]{1,0:T(8,128)(2,1)S(1)} %collective-permute-done.45.theirs, ...), custom_call_target="tpu_custom_call" | custom-call | flops 4000000000 | bytes 6291456 | tf_op jit(solution)/shard_map/head_block/pallas_call | solution.py:231
  178.1 7.7 %collective-permute-start.49 = (bf16[64,4096]{1,0:T(8,128)(2,1)S(1)}, bf16[64,4096]{1,0:T(8,128)(2,1)S(1)}, u32[]{:S(2)}, u32[]{:S(2)}) collective-permute-start(bf16[64,4096]{1,0:T(8,128)(2,1)S(1)} %constant_dynamic-update-slice_fusion.4.mine), channel_id=1, source_target_pairs={{0,1},{1,0},{2,3},{3,2},{4,5},{5,4},{6,7},{7,6},{8,9},{9,8},{10,11... | collective-permute-start | bytes 1572872 | tf_op jit(solution)/shard_map/head1/ppermute | solution.py:31
  185.7 1.5 collective-permute-done.49.theirs
  187.3 2.4 %head_block.3 = (f32[128,768]{1,0:T(8,128)S(1)}, f32[8,128]{1,0:T(8,128)S(1)}, f32[2,64,64]{2,1,0:T(8,128)S(1)}) custom-call(s32[2]{0:T(128)S(1)} %pad_add_fusion.at_ref, bf16[64,4096]{1,0:T(8,128)(2,1)S(1)} %constant_dynamic-update-slice_fusion.4.mine, bf16[64,4096]{1,0:T(8,128)(2,1)S(1)} %collective-permute-done.49.theirs, ...), custom_call_target="tpu_custom_call" | custom-call | flops 4000000000 | bytes 6291456 | tf_op jit(solution)/shard_map/head1/head_block/pallas_call | solution.py:231
  189.7 14.2 %all_to_all.15 = f32[32,3,256]{2,1,0:T(4,128)S(1)} all-to-all(f32[32,3,256]{2,1,0:T(4,128)S(1)} %broadcast_in_dim.19), channel_id=1, replica_groups=mesh['dp'=8,'pipe'=4,'tensor'=8] {'pipe','tensor'}, dimensions={0} | all-to-all | bytes 196608 | tf_op jit(solution)/shard_map/scores/all_to_all | solution.py:24
  205.4 3.8 %all-to-all-start.2 = ((f32[32,1,4]{2,1,0:T(1,128)}), f32[32,1,4]{2,1,0:T(1,128)S(1)}, u32[]{:S(2)}, u32[]{:S(2)}) async-start(f32[32,1,4]{2,1,0:T(1,128)} %broadcast_in_dim.21), calls=%async_computation.2 | async-start | bytes 32768 | tf_op jit(solution)/shard_map/scores/all_to_all | solution.py:24
  210.0 6.3 %all-to-all-done.2 = f32[32,1,4]{2,1,0:T(1,128)S(1)} async-done(((f32[32,1,4]{2,1,0:T(1,128)}), f32[32,1,4]{2,1,0:T(1,128)S(1)}, u32[]{:S(2)}, u32[]{:S(2)}) %all-to-all-start.2) | async-done | bytes 544 | tf_op jit(solution)/shard_map/scores/all_to_all | solution.py:24
  (121 shorter events, 26.3 us)
Async XLA Ops:
  0.6 18.4 %collective-permute-start.1 = (bf16[4096,256]{1,0:T(8,128)(2,1)}, bf16[4096,256]{1,0:T(8,128)(2,1)S(1)}, u32[]{:S(2)}, u32[]{:S(2)}) collective-permute-start(bf16[4096,256]{1,0:T(8,128)(2,1)} %bitcast.39), channel_id=1, source_target_pairs={{0,1},{1,0},{2,3},{3,2},{4,5},{5,4},{6,7},{7,6},{8,9},{9,8},{10,11... | collective-permute-start | bytes 6291464 | tf_op jit(solution)/shard_map/ppermute | solution.py:31
  3.9 15.2 %collective-permute-start.4 = (bf16[256,4096]{1,0:T(8,128)(2,1)}, bf16[256,4096]{1,0:T(8,128)(2,1)}, u32[]{:S(2)}, u32[]{:S(2)}) collective-permute-start(bf16[256,4096]{1,0:T(8,128)(2,1)} %bitcast.41), channel_id=1, source_target_pairs={{0,1},{1,0},{2,3},{3,2},{4,5},{5,4},{6,7},{7,6},{8,9},{9,8},{10,11... | collective-permute-start | bytes 6291464 | tf_op jit(solution)/shard_map/ppermute | solution.py:31
  5.9 13.2 %all-to-all-start = ((bf16[8,8,4096]{2,1,0:T(8,128)(2,1)}), bf16[8,8,4096]{2,1,0:T(8,128)(2,1)S(1)}, u32[]{:S(2)}, u32[]{:S(2)}) async-start(bf16[8,8,4096]{2,1,0:T(8,128)(2,1)} %bitcast.4), calls=%async_computation | async-start | bytes 1048576 | tf_op jit(solution)/shard_map/all_to_all | solution.py:304
  9.7 9.4 %collective-permute-start.2 = (bf16[4096,128]{1,0:T(8,128)(2,1)}, bf16[4096,128]{1,0:T(8,128)(2,1)}, u32[]{:S(2)}, u32[]{:S(2)}) collective-permute-start(bf16[4096,128]{1,0:T(8,128)(2,1)} %bitcast.43), channel_id=1, source_target_pairs={{0,1},{1,0},{2,3},{3,2},{4,5},{5,4},{6,7},{7,6},{8,9},{9,8},{10,11... | collective-permute-start | bytes 3145736 | tf_op jit(solution)/shard_map/ppermute | solution.py:31
  9.8 9.2 %collective-permute-start.3 = (bf16[4096,128]{1,0:T(8,128)(2,1)}, bf16[4096,128]{1,0:T(8,128)(2,1)}, u32[]{:S(2)}, u32[]{:S(2)}) collective-permute-start(bf16[4096,128]{1,0:T(8,128)(2,1)} %bitcast.45), channel_id=1, source_target_pairs={{0,1},{1,0},{2,3},{3,2},{4,5},{5,4},{6,7},{7,6},{8,9},{9,8},{10,11... | collective-permute-start | bytes 3145736 | tf_op jit(solution)/shard_map/ppermute | solution.py:31
  19.0 6.1 %copy-start = (f32[1,4096]{1,0:T(1,128)S(1)}, f32[1,4096]{1,0:T(1,128)}, u32[]{:S(2)}) copy-start(f32[1,4096]{1,0:T(1,128)} %gain_ref.1) | copy-start | bytes 49156
  19.1 1.3 copy-start.1
  25.1 23.4 %slice-start = ((s8[6291456]{0:T(1024)(128)(4,1)}), s8[4194304]{0:T(1024)(128)(4,1)S(1)}, s32[]{:S(2)}) async-start(s8[6291456]{0:T(1024)(128)(4,1)} %bitcast.31), calls=%async_computation.3 | async-start | bytes 8388608
  25.2 23.4 %slice-start.1 = ((s8[6291456]{0:T(1024)(128)(4,1)}), s8[2097152]{0:T(1024)(128)(4,1)S(1)}, s32[]{:S(2)}) async-start(s8[6291456]{0:T(1024)(128)(4,1)} %bitcast.31), calls=%async_computation.4 | async-start | bytes 4194304
  29.7 3.9 %collective-permute-start.5 = (bf16[16,4096]{1,0:T(8,128)(2,1)S(1)}, bf16[16,4096]{1,0:T(8,128)(2,1)S(1)}, u32[]{:S(2)}, u32[]{:S(2)}) collective-permute-start(bf16[16,4096]{1,0:T(8,128)(2,1)S(1)} %get-tuple-element.120), channel_id=1, source_target_pairs={{0,2},{1,3},{2,0},{3,1},{4,6},{5,7},{6,4},{7,5},{8,10},{9,11},{10,... | collective-permute-start | bytes 393224 | tf_op jit(solution)/shard_map/tick0/ppermute | solution.py:36
  30.0 6.9 %collective-permute-start.6 = (bf16[16,4096]{1,0:T(8,128)(2,1)S(1)}, bf16[16,4096]{1,0:T(8,128)(2,1)S(1)}, u32[]{:S(2)}, u32[]{:S(2)}) collective-permute-start(bf16[16,4096]{1,0:T(8,128)(2,1)S(1)} %get-tuple-element.121), channel_id=1, source_target_pairs={{0,4},{1,5},{2,6},{3,7},{4,0},{5,1},{6,2},{7,3},{8,12},{9,13},{10,... | collective-permute-start | bytes 393224 | tf_op jit(solution)/shard_map/tick0/ppermute | solution.py:36
  31.8 8.0 %collective-permute-start.7 = (bf16[16,4096]{1,0:T(8,128)(2,1)S(1)}, bf16[16,4096]{1,0:T(8,128)(2,1)S(1)}, u32[]{:S(2)}, u32[]{:S(2)}) collective-permute-start(bf16[16,4096]{1,0:T(8,128)(2,1)S(1)} %get-tuple-element.122), channel_id=1, source_target_pairs={{0,6},{1,7},{2,4},{3,5},{4,2},{5,3},{6,0},{7,1},{8,14},{9,15},{10,... | collective-permute-start | bytes 393224 | tf_op jit(solution)/shard_map/tick0/ppermute | solution.py:36
  39.9 5.0 %collective-permute-start.8 = (bf16[16,4096]{1,0:T(8,128)(2,1)S(1)}, bf16[16,4096]{1,0:T(8,128)(2,1)S(1)}, u32[]{:S(2)}, u32[]{:S(2)}) collective-permute-start(bf16[16,4096]{1,0:T(8,128)(2,1)S(1)} %add_convert_fusion.4), channel_id=1, source_target_pairs={{0,8},{8,16},{16,24},{1,9},{9,17},{17,25},{2,10},{10,18},{18,26},{... | collective-permute-start | bytes 393224 | tf_op jit(solution)/shard_map/hop1/ppermute | solution.py:41
  42.4 2.5 %collective-permute-start = (bf16[1,8,4096]{2,1,0:T(8,128)(2,1)S(1)}, bf16[1,8,4096]{2,1,0:T(8,128)(2,1)S(1)}, u32[]{:S(2)}, u32[]{:S(2)}) collective-permute-start(bf16[1,8,4096]{2,1,0:T(8,128)(2,1)S(1)} %get-tuple-element.218), channel_id=1, source_target_pairs={{0,1},{1,0},{2,3},{3,2},{4,5},{5,4},{6,7},{7,6},{8,9},{9,8},{10,11... | collective-permute-start | bytes 196616 | tf_op jit(solution)/shard_map/ppermute | solution.py:31
  45.2 5.1 %collective-permute-start.11 = (bf16[16,4096]{1,0:T(8,128)(2,1)S(1)}, bf16[16,4096]{1,0:T(8,128)(2,1)S(1)}, u32[]{:S(2)}, u32[]{:S(2)}) collective-permute-start(bf16[16,4096]{1,0:T(8,128)(2,1)S(1)} %fusion.2.r0), channel_id=1, source_target_pairs={{0,6},{1,7},{2,4},{3,5},{4,2},{5,3},{6,0},{7,1},{8,14},{9,15},{10,... | collective-permute-start | bytes 393224 | tf_op jit(solution)/shard_map/tick1/ppermute | solution.py:36
  47.1 5.4 %collective-permute-start.10 = (bf16[16,4096]{1,0:T(8,128)(2,1)S(1)}, bf16[16,4096]{1,0:T(8,128)(2,1)S(1)}, u32[]{:S(2)}, u32[]{:S(2)}) collective-permute-start(bf16[16,4096]{1,0:T(8,128)(2,1)S(1)} %fusion.2.r0), channel_id=1, source_target_pairs={{0,4},{1,5},{2,6},{3,7},{4,0},{5,1},{6,2},{7,3},{8,12},{9,13},{10,... | collective-permute-start | bytes 393224 | tf_op jit(solution)/shard_map/tick1/ppermute | solution.py:36
  47.1 6.2 %collective-permute-start.9 = (bf16[16,4096]{1,0:T(8,128)(2,1)S(1)}, bf16[16,4096]{1,0:T(8,128)(2,1)S(1)}, u32[]{:S(2)}, u32[]{:S(2)}) collective-permute-start(bf16[16,4096]{1,0:T(8,128)(2,1)S(1)} %fusion.2.r0), channel_id=1, source_target_pairs={{0,2},{1,3},{2,0},{3,1},{4,6},{5,7},{6,4},{7,5},{8,10},{9,11},{10,... | collective-permute-start | bytes 393224 | tf_op jit(solution)/shard_map/tick1/ppermute | solution.py:36
  56.9 3.9 %collective-permute-start.12 = (bf16[16,4096]{1,0:T(8,128)(2,1)S(1)}, bf16[16,4096]{1,0:T(8,128)(2,1)S(1)}, u32[]{:S(2)}, u32[]{:S(2)}) collective-permute-start(bf16[16,4096]{1,0:T(8,128)(2,1)S(1)} %get-tuple-element.133), channel_id=1, source_target_pairs={{0,2},{1,3},{2,0},{3,1},{4,6},{5,7},{6,4},{7,5},{8,10},{9,11},{10,... | collective-permute-start | bytes 393224 | tf_op jit(solution)/shard_map/tick1/ppermute | solution.py:36
  57.3 6.4 %collective-permute-start.13 = (bf16[16,4096]{1,0:T(8,128)(2,1)S(1)}, bf16[16,4096]{1,0:T(8,128)(2,1)S(1)}, u32[]{:S(2)}, u32[]{:S(2)}) collective-permute-start(bf16[16,4096]{1,0:T(8,128)(2,1)S(1)} %get-tuple-element.134), channel_id=1, source_target_pairs={{0,4},{1,5},{2,6},{3,7},{4,0},{5,1},{6,2},{7,3},{8,12},{9,13},{10,... | collective-permute-start | bytes 393224 | tf_op jit(solution)/shard_map/tick1/ppermute | solution.py:36
  59.9 5.2 %collective-permute-start.14 = (bf16[16,4096]{1,0:T(8,128)(2,1)S(1)}, bf16[16,4096]{1,0:T(8,128)(2,1)S(1)}, u32[]{:S(2)}, u32[]{:S(2)}) collective-permute-start(bf16[16,4096]{1,0:T(8,128)(2,1)S(1)} %get-tuple-element.135), channel_id=1, source_target_pairs={{0,6},{1,7},{2,4},{3,5},{4,2},{5,3},{6,0},{7,1},{8,14},{9,15},{10,... | collective-permute-start | bytes 393224 | tf_op jit(solution)/shard_map/tick1/ppermute | solution.py:36
  65.2 4.4 %collective-permute-start.15 = (bf16[16,4096]{1,0:T(8,128)(2,1)S(1)}, bf16[16,4096]{1,0:T(8,128)(2,1)S(1)}, u32[]{:S(2)}, u32[]{:S(2)}) collective-permute-start(bf16[16,4096]{1,0:T(8,128)(2,1)S(1)} %add_convert_fusion.3), channel_id=1, source_target_pairs={{0,8},{8,16},{16,24},{1,9},{9,17},{17,25},{2,10},{10,18},{18,26},{... | collective-permute-start | bytes 393224 | tf_op jit(solution)/shard_map/hop2/ppermute | solution.py:41
  69.8 5.1 %collective-permute-start.18 = (bf16[16,4096]{1,0:T(8,128)(2,1)S(1)}, bf16[16,4096]{1,0:T(8,128)(2,1)S(1)}, u32[]{:S(2)}, u32[]{:S(2)}) collective-permute-start(bf16[16,4096]{1,0:T(8,128)(2,1)S(1)} %fusion.5.r0), channel_id=1, source_target_pairs={{0,6},{1,7},{2,4},{3,5},{4,2},{5,3},{6,0},{7,1},{8,14},{9,15},{10,... | collective-permute-start | bytes 393224 | tf_op jit(solution)/shard_map/tick2/ppermute | solution.py:36
  70.9 5.4 %collective-permute-start.17 = (bf16[16,4096]{1,0:T(8,128)(2,1)S(1)}, bf16[16,4096]{1,0:T(8,128)(2,1)S(1)}, u32[]{:S(2)}, u32[]{:S(2)}) collective-permute-start(bf16[16,4096]{1,0:T(8,128)(2,1)S(1)} %fusion.5.r0), channel_id=1, source_target_pairs={{0,4},{1,5},{2,6},{3,7},{4,0},{5,1},{6,2},{7,3},{8,12},{9,13},{10,... | collective-permute-start | bytes 393224 | tf_op jit(solution)/shard_map/tick2/ppermute | solution.py:36
  72.1 4.8 %collective-permute-start.16 = (bf16[16,4096]{1,0:T(8,128)(2,1)S(1)}, bf16[16,4096]{1,0:T(8,128)(2,1)S(1)}, u32[]{:S(2)}, u32[]{:S(2)}) collective-permute-start(bf16[16,4096]{1,0:T(8,128)(2,1)S(1)} %fusion.5.r0), channel_id=1, source_target_pairs={{0,2},{1,3},{2,0},{3,1},{4,6},{5,7},{6,4},{7,5},{8,10},{9,11},{10,... | collective-permute-start | bytes 393224 | tf_op jit(solution)/shard_map/tick2/ppermute | solution.py:36
  80.5 4.6 %collective-permute-start.19 = (bf16[16,4096]{1,0:T(8,128)(2,1)S(1)}, bf16[16,4096]{1,0:T(8,128)(2,1)S(1)}, u32[]{:S(2)}, u32[]{:S(2)}) collective-permute-start(bf16[16,4096]{1,0:T(8,128)(2,1)S(1)} %get-tuple-element.144), channel_id=1, source_target_pairs={{0,2},{1,3},{2,0},{3,1},{4,6},{5,7},{6,4},{7,5},{8,10},{9,11},{10,... | collective-permute-start | bytes 393224 | tf_op jit(solution)/shard_map/tick2/ppermute | solution.py:36
  81.0 6.3 %collective-permute-start.20 = (bf16[16,4096]{1,0:T(8,128)(2,1)S(1)}, bf16[16,4096]{1,0:T(8,128)(2,1)S(1)}, u32[]{:S(2)}, u32[]{:S(2)}) collective-permute-start(bf16[16,4096]{1,0:T(8,128)(2,1)S(1)} %get-tuple-element.145), channel_id=1, source_target_pairs={{0,4},{1,5},{2,6},{3,7},{4,0},{5,1},{6,2},{7,3},{8,12},{9,13},{10,... | collective-permute-start | bytes 393224 | tf_op jit(solution)/shard_map/tick2/ppermute | solution.py:36
  82.8 5.8 %collective-permute-start.21 = (bf16[16,4096]{1,0:T(8,128)(2,1)S(1)}, bf16[16,4096]{1,0:T(8,128)(2,1)S(1)}, u32[]{:S(2)}, u32[]{:S(2)}) collective-permute-start(bf16[16,4096]{1,0:T(8,128)(2,1)S(1)} %get-tuple-element.146), channel_id=1, source_target_pairs={{0,6},{1,7},{2,4},{3,5},{4,2},{5,3},{6,0},{7,1},{8,14},{9,15},{10,... | collective-permute-start | bytes 393224 | tf_op jit(solution)/shard_map/tick2/ppermute | solution.py:36
  88.6 6.0 %collective-permute-start.22 = (bf16[16,4096]{1,0:T(8,128)(2,1)S(1)}, bf16[16,4096]{1,0:T(8,128)(2,1)S(1)}, u32[]{:S(2)}, u32[]{:S(2)}) collective-permute-start(bf16[16,4096]{1,0:T(8,128)(2,1)S(1)} %add_convert_fusion.2), channel_id=1, source_target_pairs={{0,8},{8,16},{16,24},{1,9},{9,17},{17,25},{2,10},{10,18},{18,26},{... | collective-permute-start | bytes 393224 | tf_op jit(solution)/shard_map/hop3/ppermute | solution.py:41
  94.9 26.7 %copy-start.2 = (f32[4096]{0:T(1024)S(1)}, f32[4096]{0:T(1024)}, u32[]{:S(2)}) copy-start(f32[4096]{0:T(1024)} %param.16) | copy-start | bytes 49156
  94.9 5.1 %collective-permute-start.25 = (bf16[16,4096]{1,0:T(8,128)(2,1)S(1)}, bf16[16,4096]{1,0:T(8,128)(2,1)S(1)}, u32[]{:S(2)}, u32[]{:S(2)}) collective-permute-start(bf16[16,4096]{1,0:T(8,128)(2,1)S(1)} %fusion.8.r0), channel_id=1, source_target_pairs={{0,6},{1,7},{2,4},{3,5},{4,2},{5,3},{6,0},{7,1},{8,14},{9,15},{10,... | collective-permute-start | bytes 393224 | tf_op jit(solution)/shard_map/tick3/ppermute | solution.py:36
  96.7 5.3 %collective-permute-start.24 = (bf16[16,4096]{1,0:T(8,128)(2,1)S(1)}, bf16[16,4096]{1,0:T(8,128)(2,1)S(1)}, u32[]{:S(2)}, u32[]{:S(2)}) collective-permute-start(bf16[16,4096]{1,0:T(8,128)(2,1)S(1)} %fusion.8.r0), channel_id=1, source_target_pairs={{0,4},{1,5},{2,6},{3,7},{4,0},{5,1},{6,2},{7,3},{8,12},{9,13},{10,... | collective-permute-start | bytes 393224 | tf_op jit(solution)/shard_map/tick3/ppermute | solution.py:36
  96.7 5.4 %collective-permute-start.23 = (bf16[16,4096]{1,0:T(8,128)(2,1)S(1)}, bf16[16,4096]{1,0:T(8,128)(2,1)S(1)}, u32[]{:S(2)}, u32[]{:S(2)}) collective-permute-start(bf16[16,4096]{1,0:T(8,128)(2,1)S(1)} %fusion.8.r0), channel_id=1, source_target_pairs={{0,2},{1,3},{2,0},{3,1},{4,6},{5,7},{6,4},{7,5},{8,10},{9,11},{10,... | collective-permute-start | bytes 393224 | tf_op jit(solution)/shard_map/tick3/ppermute | solution.py:36
  105.6 4.2 %collective-permute-start.26 = (bf16[16,4096]{1,0:T(8,128)(2,1)S(1)}, bf16[16,4096]{1,0:T(8,128)(2,1)S(1)}, u32[]{:S(2)}, u32[]{:S(2)}) collective-permute-start(bf16[16,4096]{1,0:T(8,128)(2,1)S(1)} %get-tuple-element.155), channel_id=1, source_target_pairs={{0,2},{1,3},{2,0},{3,1},{4,6},{5,7},{6,4},{7,5},{8,10},{9,11},{10,... | collective-permute-start | bytes 393224 | tf_op jit(solution)/shard_map/tick3/ppermute | solution.py:36
  105.7 7.6 %collective-permute-start.27 = (bf16[16,4096]{1,0:T(8,128)(2,1)S(1)}, bf16[16,4096]{1,0:T(8,128)(2,1)S(1)}, u32[]{:S(2)}, u32[]{:S(2)}) collective-permute-start(bf16[16,4096]{1,0:T(8,128)(2,1)S(1)} %get-tuple-element.156), channel_id=1, source_target_pairs={{0,4},{1,5},{2,6},{3,7},{4,0},{5,1},{6,2},{7,3},{8,12},{9,13},{10,... | collective-permute-start | bytes 393224 | tf_op jit(solution)/shard_map/tick3/ppermute | solution.py:36
  108.5 6.6 %collective-permute-start.28 = (bf16[16,4096]{1,0:T(8,128)(2,1)S(1)}, bf16[16,4096]{1,0:T(8,128)(2,1)S(1)}, u32[]{:S(2)}, u32[]{:S(2)}) collective-permute-start(bf16[16,4096]{1,0:T(8,128)(2,1)S(1)} %get-tuple-element.157), channel_id=1, source_target_pairs={{0,6},{1,7},{2,4},{3,5},{4,2},{5,3},{6,0},{7,1},{8,14},{9,15},{10,... | collective-permute-start | bytes 393224 | tf_op jit(solution)/shard_map/tick3/ppermute | solution.py:36
  115.2 6.0 %collective-permute-start.29 = (bf16[16,4096]{1,0:T(8,128)(2,1)S(1)}, bf16[16,4096]{1,0:T(8,128)(2,1)S(1)}, u32[]{:S(2)}, u32[]{:S(2)}) collective-permute-start(bf16[16,4096]{1,0:T(8,128)(2,1)S(1)} %add_convert_fusion.1), channel_id=1, source_target_pairs={{0,8},{8,16},{16,24},{1,9},{9,17},{17,25},{2,10},{10,18},{18,26},{... | collective-permute-start | bytes 393224 | tf_op jit(solution)/shard_map/hop4/ppermute | solution.py:41
  121.7 6.9 %collective-permute-start.35 = (bf16[16,4096]{1,0:T(8,128)(2,1)S(1)}, bf16[16,4096]{1,0:T(8,128)(2,1)S(1)}, u32[]{:S(2)}, u32[]{:S(2)}) collective-permute-start(bf16[16,4096]{1,0:T(8,128)(2,1)S(1)} %fusion.14), channel_id=1, source_target_pairs={{24,0},{25,1},{26,2},{27,3},{28,4},{29,5},{30,6},{31,7},{56,32},{5... | collective-permute-start | bytes 393224 | tf_op jit(solution)/shard_map/spread0/ppermute | solution.py:371
  123.0 5.6 %collective-permute-start.34 = (bf16[16,4096]{1,0:T(8,128)(2,1)S(1)}, bf16[16,4096]{1,0:T(8,128)(2,1)S(1)}, u32[]{:S(2)}, u32[]{:S(2)}) collective-permute-start(bf16[16,4096]{1,0:T(8,128)(2,1)S(1)} %fusion.14), channel_id=1, source_target_pairs={{24,8},{25,9},{26,10},{27,11},{28,12},{29,13},{30,14},{31,15},{56,... | collective-permute-start | bytes 393224 | tf_op jit(solution)/shard_map/spread0/ppermute | solution.py:371
  123.7 5.0 %collective-permute-start.33 = (bf16[16,4096]{1,0:T(8,128)(2,1)S(1)}, bf16[16,4096]{1,0:T(8,128)(2,1)S(1)}, u32[]{:S(2)}, u32[]{:S(2)}) collective-permute-start(bf16[16,4096]{1,0:T(8,128)(2,1)S(1)} %fusion.14), channel_id=1, source_target_pairs={{24,16},{25,17},{26,18},{27,19},{28,20},{29,21},{30,22},{31,23},{5... | collective-permute-start | bytes 393224 | tf_op jit(solution)/shard_map/spread0/ppermute | solution.py:371
  124.4 5.1 %collective-permute-start.32 = (bf16[16,4096]{1,0:T(8,128)(2,1)S(1)}, bf16[16,4096]{1,0:T(8,128)(2,1)S(1)}, u32[]{:S(2)}, u32[]{:S(2)}) collective-permute-start(bf16[16,4096]{1,0:T(8,128)(2,1)S(1)} %fusion.11.r0), channel_id=1, source_target_pairs={{0,6},{1,7},{2,4},{3,5},{4,2},{5,3},{6,0},{7,1},{8,14},{9,15},{10,... | collective-permute-start | bytes 393224 | tf_op jit(solution)/shard_map/tick4/ppermute | solution.py:36
  125.9 5.3 %collective-permute-start.31 = (bf16[16,4096]{1,0:T(8,128)(2,1)S(1)}, bf16[16,4096]{1,0:T(8,128)(2,1)S(1)}, u32[]{:S(2)}, u32[]{:S(2)}) collective-permute-start(bf16[16,4096]{1,0:T(8,128)(2,1)S(1)} %fusion.11.r0), channel_id=1, source_target_pairs={{0,4},{1,5},{2,6},{3,7},{4,0},{5,1},{6,2},{7,3},{8,12},{9,13},{10,... | collective-permute-start | bytes 393224 | tf_op jit(solution)/shard_map/tick4/ppermute | solution.py:36
  128.6 3.8 %collective-permute-start.30 = (bf16[16,4096]{1,0:T(8,128)(2,1)S(1)}, bf16[16,4096]{1,0:T(8,128)(2,1)S(1)}, u32[]{:S(2)}, u32[]{:S(2)}) collective-permute-start(bf16[16,4096]{1,0:T(8,128)(2,1)S(1)} %fusion.11.r0), channel_id=1, source_target_pairs={{0,2},{1,3},{2,0},{3,1},{4,6},{5,7},{6,4},{7,5},{8,10},{9,11},{10,... | collective-permute-start | bytes 393224 | tf_op jit(solution)/shard_map/tick4/ppermute | solution.py:36
  136.0 5.6 %collective-permute-start.36 = (bf16[16,4096]{1,0:T(8,128)(2,1)S(1)}, bf16[16,4096]{1,0:T(8,128)(2,1)S(1)}, u32[]{:S(2)}, u32[]{:S(2)}) collective-permute-start(bf16[16,4096]{1,0:T(8,128)(2,1)S(1)} %get-tuple-element.169), channel_id=1, source_target_pairs={{0,2},{1,3},{2,0},{3,1},{4,6},{5,7},{6,4},{7,5},{8,10},{9,11},{10,... | collective-permute-start | bytes 393224 | tf_op jit(solution)/shard_map/tick4/ppermute | solution.py:36
  136.3 7.1 %collective-permute-start.37 = (bf16[16,4096]{1,0:T(8,128)(2,1)S(1)}, bf16[16,4096]{1,0:T(8,128)(2,1)S(1)}, u32[]{:S(2)}, u32[]{:S(2)}) collective-permute-start(bf16[16,4096]{1,0:T(8,128)(2,1)S(1)} %get-tuple-element.170), channel_id=1, source_target_pairs={{0,4},{1,5},{2,6},{3,7},{4,0},{5,1},{6,2},{7,3},{8,12},{9,13},{10,... | collective-permute-start | bytes 393224 | tf_op jit(solution)/shard_map/tick4/ppermute | solution.py:36
  139.0 9.6 %collective-permute-start.38 = (bf16[16,4096]{1,0:T(8,128)(2,1)S(1)}, bf16[16,4096]{1,0:T(8,128)(2,1)S(1)}, u32[]{:S(2)}, u32[]{:S(2)}) collective-permute-start(bf16[16,4096]{1,0:T(8,128)(2,1)S(1)} %get-tuple-element.171), channel_id=1, source_target_pairs={{0,6},{1,7},{2,4},{3,5},{4,2},{5,3},{6,0},{7,1},{8,14},{9,15},{10,... | collective-permute-start | bytes 393224 | tf_op jit(solution)/shard_map/tick4/ppermute | solution.py:36
  140.2 9.5 %collective-permute-start.41 = (bf16[16,4096]{1,0:T(8,128)(2,1)S(1)}, bf16[16,4096]{1,0:T(8,128)(2,1)S(1)}, u32[]{:S(2)}, u32[]{:S(2)}) collective-permute-start(bf16[16,4096]{1,0:T(8,128)(2,1)S(1)} %select_select_fusion.1), channel_id=1, source_target_pairs={{0,6},{1,7},{2,4},{3,5},{4,2},{5,3},{6,0},{7,1},{8,14},{9,15},{10,... | collective-permute-start | bytes 393224 | tf_op jit(solution)/shard_map/tick4/ppermute | solution.py:36
  141.6 8.1 %collective-permute-start.40 = (bf16[16,4096]{1,0:T(8,128)(2,1)S(1)}, bf16[16,4096]{1,0:T(8,128)(2,1)S(1)}, u32[]{:S(2)}, u32[]{:S(2)}) collective-permute-start(bf16[16,4096]{1,0:T(8,128)(2,1)S(1)} %select_select_fusion.1), channel_id=1, source_target_pairs={{0,4},{1,5},{2,6},{3,7},{4,0},{5,1},{6,2},{7,3},{8,12},{9,13},{10,... | collective-permute-start | bytes 393224 | tf_op jit(solution)/shard_map/tick4/ppermute | solution.py:36
  141.6 8.1 %collective-permute-start.39 = (bf16[16,4096]{1,0:T(8,128)(2,1)S(1)}, bf16[16,4096]{1,0:T(8,128)(2,1)S(1)}, u32[]{:S(2)}, u32[]{:S(2)}) collective-permute-start(bf16[16,4096]{1,0:T(8,128)(2,1)S(1)} %select_select_fusion.1), channel_id=1, source_target_pairs={{0,2},{1,3},{2,0},{3,1},{4,6},{5,7},{6,4},{7,5},{8,10},{9,11},{10,... | collective-permute-start | bytes 393224 | tf_op jit(solution)/shard_map/tick4/ppermute | solution.py:36
  150.1 19.4 %collective-permute-start.44 = (bf16[16,4096]{1,0:T(8,128)(2,1)S(1)}, bf16[16,4096]{1,0:T(8,128)(2,1)S(1)}, u32[]{:S(2)}, u32[]{:S(2)}) collective-permute-start(bf16[16,4096]{1,0:T(8,128)(2,1)S(1)} %fusion.17), channel_id=1, source_target_pairs={{24,0},{25,1},{26,2},{27,3},{28,4},{29,5},{30,6},{31,7},{56,32},{5... | collective-permute-start | bytes 393224 | tf_op jit(solution)/shard_map/spread1/ppermute | solution.py:371
  151.4 18.1 %collective-permute-start.43 = (bf16[16,4096]{1,0:T(8,128)(2,1)S(1)}, bf16[16,4096]{1,0:T(8,128)(2,1)S(1)}, u32[]{:S(2)}, u32[]{:S(2)}) collective-permute-start(bf16[16,4096]{1,0:T(8,128)(2,1)S(1)} %fusion.17), channel_id=1, source_target_pairs={{24,8},{25,9},{26,10},{27,11},{28,12},{29,13},{30,14},{31,15},{56,... | collective-permute-start | bytes 393224 | tf_op jit(solution)/shard_map/spread1/ppermute | solution.py:371
  152.0 17.4 %collective-permute-start.42 = (bf16[16,4096]{1,0:T(8,128)(2,1)S(1)}, bf16[16,4096]{1,0:T(8,128)(2,1)S(1)}, u32[]{:S(2)}, u32[]{:S(2)}) collective-permute-start(bf16[16,4096]{1,0:T(8,128)(2,1)S(1)} %fusion.17), channel_id=1, source_target_pairs={{24,16},{25,17},{26,18},{27,19},{28,20},{29,21},{30,22},{31,23},{5... | collective-permute-start | bytes 393224 | tf_op jit(solution)/shard_map/spread1/ppermute | solution.py:371
  152.8 18.2 %collective-permute-start.45 = (bf16[64,4096]{1,0:T(8,128)(2,1)S(1)}, bf16[64,4096]{1,0:T(8,128)(2,1)S(1)}, u32[]{:S(2)}, u32[]{:S(2)}) collective-permute-start(bf16[64,4096]{1,0:T(8,128)(2,1)S(1)} %constant_dynamic-update-slice_fusion.mine), channel_id=1, source_target_pairs={{0,1},{1,0},{2,3},{3,2},{4,5},{5,4},{6,7},{7,6},{8,9},{9,8},{10,11... | collective-permute-start | bytes 1572872 | tf_op jit(solution)/shard_map/head0/ppermute | solution.py:31
  171.0 5.7 %collective-permute-start.48 = (bf16[16,4096]{1,0:T(8,128)(2,1)S(1)}, bf16[16,4096]{1,0:T(8,128)(2,1)S(1)}, u32[]{:S(2)}, u32[]{:S(2)}) collective-permute-start(bf16[16,4096]{1,0:T(8,128)(2,1)S(1)} %select_select_fusion), channel_id=1, source_target_pairs={{0,6},{1,7},{2,4},{3,5},{4,2},{5,3},{6,0},{7,1},{8,14},{9,15},{10,... | collective-permute-start | bytes 393224 | tf_op jit(solution)/shard_map/head1/ppermute | solution.py:36
  172.3 5.3 %collective-permute-start.47 = (bf16[16,4096]{1,0:T(8,128)(2,1)S(1)}, bf16[16,4096]{1,0:T(8,128)(2,1)S(1)}, u32[]{:S(2)}, u32[]{:S(2)}) collective-permute-start(bf16[16,4096]{1,0:T(8,128)(2,1)S(1)} %select_select_fusion), channel_id=1, source_target_pairs={{0,4},{1,5},{2,6},{3,7},{4,0},{5,1},{6,2},{7,3},{8,12},{9,13},{10,... | collective-permute-start | bytes 393224 | tf_op jit(solution)/shard_map/head1/ppermute | solution.py:36
  173.1 4.9 %collective-permute-start.46 = (bf16[16,4096]{1,0:T(8,128)(2,1)S(1)}, bf16[16,4096]{1,0:T(8,128)(2,1)S(1)}, u32[]{:S(2)}, u32[]{:S(2)}) collective-permute-start(bf16[16,4096]{1,0:T(8,128)(2,1)S(1)} %select_select_fusion), channel_id=1, source_target_pairs={{0,2},{1,3},{2,0},{3,1},{4,6},{5,7},{6,4},{7,5},{8,10},{9,11},{10,... | collective-permute-start | bytes 393224 | tf_op jit(solution)/shard_map/head1/ppermute | solution.py:36
  178.1 9.2 %collective-permute-start.49 = (bf16[64,4096]{1,0:T(8,128)(2,1)S(1)}, bf16[64,4096]{1,0:T(8,128)(2,1)S(1)}, u32[]{:S(2)}, u32[]{:S(2)}) collective-permute-start(bf16[64,4096]{1,0:T(8,128)(2,1)S(1)} %constant_dynamic-update-slice_fusion.4.mine), channel_id=1, source_target_pairs={{0,1},{1,0},{2,3},{3,2},{4,5},{5,4},{6,7},{7,6},{8,9},{9,8},{10,11... | collective-permute-start | bytes 1572872 | tf_op jit(solution)/shard_map/head1/ppermute | solution.py:31
  205.4 10.9 %all-to-all-start.2 = ((f32[32,1,4]{2,1,0:T(1,128)}), f32[32,1,4]{2,1,0:T(1,128)S(1)}, u32[]{:S(2)}, u32[]{:S(2)}) async-start(f32[32,1,4]{2,1,0:T(1,128)} %broadcast_in_dim.21), calls=%async_computation.2 | async-start | bytes 32768 | tf_op jit(solution)/shard_map/scores/all_to_all | solution.py:24
